TPU v7x, 32 devices: a whole 2x2x4 slice. The times are simulated.
32 devices in a mesh: aa: 4 (over z), ba: 8 (over y, x, core).
Axes of the slice: x: 2, y: 2, z: 4, core: 2. Of those that a mesh axis runs over, the one named last changes fastest.
Arguments:
- deltas: bfloat16 [16384, 128], P(('aa', 'ba')), may hold values from -6 to 6
- row_ids: int32 [16384], P(('aa', 'ba')), may hold values from 0 to 4095, as said below
- sample_counts: int32 [16384], P(('aa', 'ba')), may hold values from 1 to 8
- live: int32 [16384], P(('aa', 'ba')), may hold values from 0 to 1, as said below
- table: float32 [131072, 128], P(('aa', 'ba')), may hold values from -6 to 6
- accum: float32 [131072, 128], P(('aa', 'ba')), may hold values from 0.01 to 1
Outputs:
- new_table: float32 [131072, 128], P(('aa', 'ba'))
- new_accum: float32 [131072, 128], P(('aa', 'ba'))
- fresh_rows: bfloat16 [16384, 128], P(('aa', 'ba'))
Inputs may be any that keep to these rules, and one draw needn't show every extreme that they name: `row_ids`: A replica's 512 slots are 32 blocks of 16; block j holds rows of owner j, given as offsets among its 4096 rows, pairwise distinct within the block. In each block of 16 slots the live ones come first; every replica has some block with all 16 slots live.
All inputs are finite; a program needn't handle non-finite values.
Results may differ from a plain program's by a relative error of at most 0.0012.
Values may be sent and summed in bfloat16 or wider, within the bound.
No kernel may reach another device: no remote copies, remote signals or barrier semaphores. Data moves between devices by JAX's collectives and lax.ppermute only.
A program may use at most 64 MiB of HBM per device.

v0:
```python
import jax
import jax.numpy as jnp
from jax import lax
from jax.sharding import PartitionSpec as P

learn_rate = 0.1
epsilon = 1e-08


def on_device(deltas, row_ids, sample_counts, live, table, accum):
    n_first = lax.axis_size("aa")
    n_second = lax.axis_size("ba")
    width = deltas.shape[1]
    rows_owned = table.shape[0]
    slot_cap = deltas.shape[0] // (n_first * n_second)
    grid = (n_first, n_second, slot_cap)
    blocks = deltas.reshape(n_first, n_second, slot_cap, width)
    ids = row_ids.reshape(grid)
    payload = (blocks, ids, (sample_counts * live).reshape(grid))
    arrived = (
        lax.all_to_all(
            lax.all_to_all(payload[0], "aa", split_axis=0, concat_axis=0, tiled=True),
            "ba",
            split_axis=1,
            concat_axis=1,
            tiled=True,
        ),
        lax.all_to_all(
            lax.all_to_all(payload[1], "aa", split_axis=0, concat_axis=0, tiled=True),
            "ba",
            split_axis=1,
            concat_axis=1,
            tiled=True,
        ),
        lax.all_to_all(
            lax.all_to_all(payload[2], "aa", split_axis=0, concat_axis=0, tiled=True),
            "ba",
            split_axis=1,
            concat_axis=1,
            tiled=True,
        ),
    )
    got_rows, got_ids, got_weight = arrived
    local = got_ids.reshape(-1).astype(jnp.int32)
    weight = got_weight.reshape(-1).astype(jnp.float32)
    slot_rows = got_rows.reshape(-1, width)
    block_len = min(512, rows_owned)
    n_blocks = rows_owned // block_len
    table_blocks = table.reshape(n_blocks, block_len, width)
    accum_blocks = accum.reshape(n_blocks, block_len, width)
    offsets = jnp.arange(n_blocks, dtype=jnp.int32) * block_len
    within = jnp.arange(block_len, dtype=jnp.int32)
    contract = (((0,), (0,)), ((), ()))

    def owner_block(replies, inputs):
        start, table_part, accum_part = inputs
        matched = local[:, None] == (start + within)[None, :]
        weighted = jnp.where(matched, weight[:, None], 0.0)
        numer = lax.dot_general(
            weighted.astype(jnp.bfloat16), slot_rows, contract, preferred_element_type=jnp.float32
        )
        total = jnp.sum(weighted, axis=0)
        grad = numer / jnp.maximum(total, 1.0)[:, None]
        accum_next = accum_part + grad * grad
        table_next = table_part - learn_rate * grad / (jnp.sqrt(accum_next) + epsilon)
        upper = table_next.astype(jnp.bfloat16)
        lower = (table_next - upper.astype(jnp.float32)).astype(jnp.bfloat16)
        picker = matched.astype(jnp.bfloat16)
        picked = jnp.dot(picker, upper, preferred_element_type=jnp.float32) + jnp.dot(
            picker, lower, preferred_element_type=jnp.float32
        )
        return (replies + picked, (table_next, accum_next))

    start_replies = jnp.zeros((local.shape[0], width), jnp.float32)
    gathered, updated = lax.scan(owner_block, start_replies, (offsets, table_blocks, accum_blocks))
    new_table = updated[0].reshape(rows_owned, width)
    new_accum = updated[1].reshape(rows_owned, width)
    replies = gathered.astype(jnp.bfloat16).reshape(n_first, n_second, slot_cap, width)
    returned = lax.all_to_all(
        lax.all_to_all(replies, "aa", split_axis=0, concat_axis=0, tiled=True),
        "ba",
        split_axis=1,
        concat_axis=1,
        tiled=True,
    )
    return (new_table, new_accum, returned.reshape(-1, width))


def solution(mesh):
    placed = (
        P(("aa", "ba"), None),
        P(("aa", "ba")),
        P(("aa", "ba")),
        P(("aa", "ba")),
        P(("aa", "ba"), None),
        P(("aa", "ba"), None),
    )
    return jax.shard_map(
        on_device,
        mesh=mesh,
        in_specs=placed,
        out_specs=(P(("aa", "ba"), None), P(("aa", "ba"), None), P(("aa", "ba"), None)),
        check_vma=False,
    )
```

profile of v0, /device:TPU:0, one launch (start us, length us, event | category | flops | bytes accessed | tf_op | source)
XLA Modules:
  0.0 111.1 jit_solution(17680184323755228540)
XLA Ops:
  0.6 0.8 reshape.46
  1.4 0.7 reshape.56
  2.1 6.3 %all-to-all-start = ((s32[4,1,128]{2,1,0:T(1,128)}), s32[4,1,128]{2,1,0:T(1,128)S(1)}, u32[]{:S(2)}, u32[]{:S(2)}) async-start(s32[4,1,128]{2,1,0:T(1,128)} %reshape.56), calls=%async_computation | async-start | bytes 4096 | tf_op jit(solution)/shard_map/all_to_all | solution.py:29
  8.4 0.7 mul.13
  9.2 0.7 reshape.58
  9.8 4.1 %all-to-all-done = s32[4,1,128]{2,1,0:T(1,128)S(1)} async-done(((s32[4,1,128]{2,1,0:T(1,128)}), s32[4,1,128]{2,1,0:T(1,128)S(1)}, u32[]{:S(2)}, u32[]{:S(2)}) %all-to-all-start) | async-done | bytes 2080 | tf_op jit(solution)/shard_map/all_to_all | solution.py:29
  13.9 3.2 %all-to-all-start.2 = ((s32[4,1,128]{2,1,0:T(1,128)}), s32[4,1,128]{2,1,0:T(1,128)S(1)}, u32[]{:S(2)}, u32[]{:S(2)}) async-start(s32[4,1,128]{2,1,0:T(1,128)} %reshape.58), calls=%async_computation.2 | async-start | bytes 4096 | tf_op jit(solution)/shard_map/all_to_all | solution.py:36
  17.1 0.5 broadcast.41
  17.6 0.7 reduce
  18.4 4.2 %all-to-all-done.2 = s32[4,1,128]{2,1,0:T(1,128)S(1)} async-done(((s32[4,1,128]{2,1,0:T(1,128)}), s32[4,1,128]{2,1,0:T(1,128)S(1)}, u32[]{:S(2)}, u32[]{:S(2)}) %all-to-all-start.2) | async-done | bytes 2080 | tf_op jit(solution)/shard_map/all_to_all | solution.py:36
  22.6 8.3 %all_to_all.40 = s32[4,8,16]{2,0,1:T(4,128)S(1)} all-to-all(s32[4,8,16]{2,0,1:T(4,128)S(1)} %copy.26), channel_id=1, replica_groups=mesh['aa'=4,'ba'=8] {'ba'}, dimensions={1} | all-to-all | bytes 4096 | tf_op jit(solution)/shard_map/all_to_all | solution.py:28
  30.9 3.3 %all-to-all-start.4 = ((bf16[4,8,16,128]{3,2,1,0:T(8,128)(2,1)}), bf16[4,8,16,128]{3,2,1,0:T(8,128)(2,1)S(1)}, u32[]{:S(2)}, u32[]{:S(2)}) async-start(bf16[4,8,16,128]{3,2,1,0:T(8,128)(2,1)} %bitcast.34), calls=%async_computation.4 | async-start | bytes 262144 | tf_op jit(solution)/shard_map/all_to_all | solution.py:22
  34.2 0.7 reduce.1
  34.9 0.6 copy.27
  35.5 4.7 %all-to-all-done.4 = bf16[4,8,16,128]{3,2,1,0:T(8,128)(2,1)S(1)} async-done(((bf16[4,8,16,128]{3,2,1,0:T(8,128)(2,1)}), bf16[4,8,16,128]{3,2,1,0:T(8,128)(2,1)S(1)}, u32[]{:S(2)}, u32[]{:S(2)}) %all-to-all-start.4) | async-done | bytes 131104 | tf_op jit(solution)/shard_map/all_to_all | solution.py:22
  40.3 3.3 %all-to-all-start.3 = ((s32[4,8,16]{2,0,1:T(4,128)}), s32[4,8,16]{2,0,1:T(4,128)S(1)}, u32[]{:S(2)}, u32[]{:S(2)}) async-start(s32[4,8,16]{2,0,1:T(4,128)} %copy.27), calls=%async_computation.3 | async-start | bytes 32768 | tf_op jit(solution)/shard_map/all_to_all | solution.py:35
  43.8 0.7 copy.29
  44.4 3.9 %all-to-all-done.3 = s32[4,8,16]{2,0,1:T(4,128)S(1)} async-done(((s32[4,8,16]{2,0,1:T(4,128)}), s32[4,8,16]{2,0,1:T(4,128)S(1)}, u32[]{:S(2)}, u32[]{:S(2)}) %all-to-all-start.3) | async-done | bytes 2080 | tf_op jit(solution)/shard_map/all_to_all | solution.py:35
  48.3 3.4 %all-to-all-start.5 = ((bf16[4,8,16,128]{3,2,0,1:T(8,128)(2,1)}), bf16[4,8,16,128]{3,2,0,1:T(8,128)(2,1)S(1)}, u32[]{:S(2)}, u32[]{:S(2)}) async-start(bf16[4,8,16,128]{3,2,0,1:T(8,128)(2,1)} %copy.29), calls=%async_computation.5 | async-start | bytes 262144 | tf_op jit(solution)/shard_map/all_to_all | solution.py:21
  51.8 5.3 %all-to-all-done.5 = bf16[4,8,16,128]{3,2,0,1:T(8,128)(2,1)S(1)} async-done(((bf16[4,8,16,128]{3,2,0,1:T(8,128)(2,1)}), bf16[4,8,16,128]{3,2,0,1:T(8,128)(2,1)S(1)}, u32[]{:S(2)}, u32[]{:S(2)}) %all-to-all-start.5) | async-done | bytes 131104 | tf_op jit(solution)/shard_map/all_to_all | solution.py:21
  57.2 36.7 %while.16 = (s32[]{:T(128)}, f32[512,128]{1,0:T(8,128)S(1)}, f32[8,512,128]{2,1,0:T(8,128)}, f32[8,512,128]{2,1,0:T(8,128)}, s32[4,8,16]{2,1,0:T(8,128)}, /*inde...) while((s32[]{:T(128)}, f32[512,128]{1,0:T(8,128)S(1)}, ...), condition=%wide.wide.region_2.3_spmd.clone, body=%wide.wide.region_0.2_spmd.clone.sunk | while | flops 204145152 | bytes 3046039 | solution.py:75
  57.2 0.6 dynamic_slice.24
  57.8 0.6 iota_add_fusion.3
  58.6 2.4 %bitcast_dynamic-update-slice_fusion.4 = (f32[8,512,128]{2,1,0:T(8,128)}, f32[512,128]{1,0:T(8,128)S(1)}, f32[8,512,128]{2,1,0:T(8,128)}) fusion(f32[8,512,128]{2,1,0:T(8,128)} %get-tuple-element.294, s32[]{:T(128)} %get-tuple-element.292, f32[8,512,128]{2,1,0:T(8,128)} %get-tuple-element.314, f32[8,512,128]{2,1,0:T(8,128)} %get-tuple-element.311, ...), kind=kOutput, calls=%fused_computation.20.clone.clone.1 | convolution fusion | flops 68091904 | bytes 1450496 | tf_op jit(solution)/shard_map/while/body/eval_jaxpr/dot_general | solution.py:59
  61.8 0.6 dynamic_slice.24
  62.4 0.6 iota_add_fusion.3
  63.2 2.4 %bitcast_dynamic-update-slice_fusion.4 = (f32[8,512,128]{2,1,0:T(8,128)}, f32[512,128]{1,0:T(8,128)S(1)}, f32[8,512,128]{2,1,0:T(8,128)}) fusion(f32[8,512,128]{2,1,0:T(8,128)} %get-tuple-element.294, s32[]{:T(128)} %get-tuple-element.292, f32[8,512,128]{2,1,0:T(8,128)} %get-tuple-element.314, f32[8,512,128]{2,1,0:T(8,128)} %get-tuple-element.311, ...), kind=kOutput, calls=%fused_computation.20.clone.clone.1 | convolution fusion | flops 68091904 | bytes 1450496 | tf_op jit(solution)/shard_map/while/body/eval_jaxpr/dot_general | solution.py:59
  66.4 0.6 dynamic_slice.24
  66.9 0.6 iota_add_fusion.3
  67.8 2.4 %bitcast_dynamic-update-slice_fusion.4 = (f32[8,512,128]{2,1,0:T(8,128)}, f32[512,128]{1,0:T(8,128)S(1)}, f32[8,512,128]{2,1,0:T(8,128)}) fusion(f32[8,512,128]{2,1,0:T(8,128)} %get-tuple-element.294, s32[]{:T(128)} %get-tuple-element.292, f32[8,512,128]{2,1,0:T(8,128)} %get-tuple-element.314, f32[8,512,128]{2,1,0:T(8,128)} %get-tuple-element.311, ...), kind=kOutput, calls=%fused_computation.20.clone.clone.1 | convolution fusion | flops 68091904 | bytes 1450496 | tf_op jit(solution)/shard_map/while/body/eval_jaxpr/dot_general | solution.py:59
  70.9 0.6 dynamic_slice.24
  71.5 0.6 iota_add_fusion.3
  72.4 2.4 %bitcast_dynamic-update-slice_fusion.4 = (f32[8,512,128]{2,1,0:T(8,128)}, f32[512,128]{1,0:T(8,128)S(1)}, f32[8,512,128]{2,1,0:T(8,128)}) fusion(f32[8,512,128]{2,1,0:T(8,128)} %get-tuple-element.294, s32[]{:T(128)} %get-tuple-element.292, f32[8,512,128]{2,1,0:T(8,128)} %get-tuple-element.314, f32[8,512,128]{2,1,0:T(8,128)} %get-tuple-element.311, ...), kind=kOutput, calls=%fused_computation.20.clone.clone.1 | convolution fusion | flops 68091904 | bytes 1450496 | tf_op jit(solution)/shard_map/while/body/eval_jaxpr/dot_general | solution.py:59
  75.5 0.6 dynamic_slice.24
  76.1 0.6 iota_add_fusion.3
  77.0 2.4 %bitcast_dynamic-update-slice_fusion.4 = (f32[8,512,128]{2,1,0:T(8,128)}, f32[512,128]{1,0:T(8,128)S(1)}, f32[8,512,128]{2,1,0:T(8,128)}) fusion(f32[8,512,128]{2,1,0:T(8,128)} %get-tuple-element.294, s32[]{:T(128)} %get-tuple-element.292, f32[8,512,128]{2,1,0:T(8,128)} %get-tuple-element.314, f32[8,512,128]{2,1,0:T(8,128)} %get-tuple-element.311, ...), kind=kOutput, calls=%fused_computation.20.clone.clone.1 | convolution fusion | flops 68091904 | bytes 1450496 | tf_op jit(solution)/shard_map/while/body/eval_jaxpr/dot_general | solution.py:59
  80.1 0.6 dynamic_slice.24
  80.7 0.6 iota_add_fusion.3
  81.6 2.4 %bitcast_dynamic-update-slice_fusion.4 = (f32[8,512,128]{2,1,0:T(8,128)}, f32[512,128]{1,0:T(8,128)S(1)}, f32[8,512,128]{2,1,0:T(8,128)}) fusion(f32[8,512,128]{2,1,0:T(8,128)} %get-tuple-element.294, s32[]{:T(128)} %get-tuple-element.292, f32[8,512,128]{2,1,0:T(8,128)} %get-tuple-element.314, f32[8,512,128]{2,1,0:T(8,128)} %get-tuple-element.311, ...), kind=kOutput, calls=%fused_computation.20.clone.clone.1 | convolution fusion | flops 68091904 | bytes 1450496 | tf_op jit(solution)/shard_map/while/body/eval_jaxpr/dot_general | solution.py:59
  84.7 0.6 dynamic_slice.24
  85.3 0.6 iota_add_fusion.3
  86.2 2.4 %bitcast_dynamic-update-slice_fusion.4 = (f32[8,512,128]{2,1,0:T(8,128)}, f32[512,128]{1,0:T(8,128)S(1)}, f32[8,512,128]{2,1,0:T(8,128)}) fusion(f32[8,512,128]{2,1,0:T(8,128)} %get-tuple-element.294, s32[]{:T(128)} %get-tuple-element.292, f32[8,512,128]{2,1,0:T(8,128)} %get-tuple-element.314, f32[8,512,128]{2,1,0:T(8,128)} %get-tuple-element.311, ...), kind=kOutput, calls=%fused_computation.20.clone.clone.1 | convolution fusion | flops 68091904 | bytes 1450496 | tf_op jit(solution)/shard_map/while/body/eval_jaxpr/dot_general | solution.py:59
  89.3 0.6 dynamic_slice.24
  89.9 0.6 iota_add_fusion.3
  90.7 2.4 %bitcast_dynamic-update-slice_fusion.4 = (f32[8,512,128]{2,1,0:T(8,128)}, f32[512,128]{1,0:T(8,128)S(1)}, f32[8,512,128]{2,1,0:T(8,128)}) fusion(f32[8,512,128]{2,1,0:T(8,128)} %get-tuple-element.294, s32[]{:T(128)} %get-tuple-element.292, f32[8,512,128]{2,1,0:T(8,128)} %get-tuple-element.314, f32[8,512,128]{2,1,0:T(8,128)} %get-tuple-element.311, ...), kind=kOutput, calls=%fused_computation.20.clone.clone.1 | convolution fusion | flops 68091904 | bytes 1450496 | tf_op jit(solution)/shard_map/while/body/eval_jaxpr/dot_general | solution.py:59
  93.9 8.6 %all_to_all.41 = bf16[4,8,16,128]{3,2,1,0:T(8,128)(2,1)S(1)} all-to-all(bf16[4,8,16,128]{3,2,1,0:T(8,128)(2,1)S(1)} %bitcast.33), channel_id=1, replica_groups=mesh['aa'=4,'ba'=8] {'aa'}, dimensions={0} | all-to-all | bytes 262144 | tf_op jit(solution)/shard_map/all_to_all | solution.py:80
  102.5 7.9 %all_to_all.42 = bf16[4,8,16,128]{3,2,0,1:T(8,128)(2,1)S(1)} all-to-all(bf16[4,8,16,128]{3,2,0,1:T(8,128)(2,1)S(1)} %copy.32), channel_id=1, replica_groups=mesh['aa'=4,'ba'=8] {'ba'}, dimensions={1} | all-to-all | bytes 262144 | tf_op jit(solution)/shard_map/all_to_all | solution.py:79
  110.4 0.7 copy.33
  (49 shorter events, 8.1 us)
Async XLA Ops:
  2.1 11.8 %all-to-all-start = ((s32[4,1,128]{2,1,0:T(1,128)}), s32[4,1,128]{2,1,0:T(1,128)S(1)}, u32[]{:S(2)}, u32[]{:S(2)}) async-start(s32[4,1,128]{2,1,0:T(1,128)} %reshape.56), calls=%async_computation | async-start | bytes 4096 | tf_op jit(solution)/shard_map/all_to_all | solution.py:29
  13.9 8.7 %all-to-all-start.2 = ((s32[4,1,128]{2,1,0:T(1,128)}), s32[4,1,128]{2,1,0:T(1,128)S(1)}, u32[]{:S(2)}, u32[]{:S(2)}) async-start(s32[4,1,128]{2,1,0:T(1,128)} %reshape.58), calls=%async_computation.2 | async-start | bytes 4096 | tf_op jit(solution)/shard_map/all_to_all | solution.py:36
  30.9 9.4 %all-to-all-start.4 = ((bf16[4,8,16,128]{3,2,1,0:T(8,128)(2,1)}), bf16[4,8,16,128]{3,2,1,0:T(8,128)(2,1)S(1)}, u32[]{:S(2)}, u32[]{:S(2)}) async-start(bf16[4,8,16,128]{3,2,1,0:T(8,128)(2,1)} %bitcast.34), calls=%async_computation.4 | async-start | bytes 262144 | tf_op jit(solution)/shard_map/all_to_all | solution.py:22
  40.3 8.0 %all-to-all-start.3 = ((s32[4,8,16]{2,0,1:T(4,128)}), s32[4,8,16]{2,0,1:T(4,128)S(1)}, u32[]{:S(2)}, u32[]{:S(2)}) async-start(s32[4,8,16]{2,0,1:T(4,128)} %copy.27), calls=%async_computation.3 | async-start | bytes 32768 | tf_op jit(solution)/shard_map/all_to_all | solution.py:35
  43.7 13.5 %copy-start = (s32[4,8,16]{2,1,0:T(8,128)}, s32[4,8,16]{2,1,0:T(8,128)S(1)}, u32[]{:S(2)}) copy-start(s32[4,8,16]{2,1,0:T(8,128)S(1)} %copy.31) | copy-start | bytes 6148
  48.3 8.8 %all-to-all-start.5 = ((bf16[4,8,16,128]{3,2,0,1:T(8,128)(2,1)}), bf16[4,8,16,128]{3,2,0,1:T(8,128)(2,1)S(1)}, u32[]{:S(2)}, u32[]{:S(2)}) async-start(bf16[4,8,16,128]{3,2,0,1:T(8,128)(2,1)} %copy.29), calls=%async_computation.5 | async-start | bytes 262144 | tf_op jit(solution)/shard_map/all_to_all | solution.py:21
where the time goes:
time: 112 us; the launch traced here: 111 us
  blocking collectives  24.8 us (22%)
  matrix products  24.7 us (22%)
  waiting for transfers between devices  22.2 us (20%)
  starting transfers between devices  19.6 us (18%)
  local copies, waits for them, and re-layouts  9.66 us (9%)
  other arithmetic  9 us (8%)
    dot_general x8, matrix products, owner_block(): lax.dot_general(weighted.astype(jnp.bfloat16), slot_rows, contract, prefe...  18.9 us
    all_to_all x1, blocking collectives, on_device(): lax.all_to_all(replies, 'aa', split_axis=0, concat_axis=0, tiled=True)  8.64 us
    all_to_all x1, blocking collectives, on_device(): lax.all_to_all(lax.all_to_all(payload[1], 'aa', split_axis=0, concat_axis...  8.26 us
    all_to_all x1, blocking collectives, on_device(): lax.all_to_all(lax.all_to_all(replies, 'aa', split_axis=0, concat_axis=0,...  7.89 us
    all_to_all x1, starting transfers between devices, on_device(): lax.all_to_all(payload[1], 'aa', split_axis=0, concat_axis=0, tiled=True)  6.35 us
    all_to_all x1, waiting for transfers between devices, on_device(): lax.all_to_all(lax.all_to_all(payload[0], 'aa', split_axis=0, concat_axis...  5.34 us
    add x8, other arithmetic, owner_block(): matched = local[:, None] == (start + within)[None, :]  5.17 us
    all_to_all x1, waiting for transfers between devices, on_device(): lax.all_to_all(payload[0], 'aa', split_axis=0, concat_axis=0, tiled=True)  4.74 us
  transfers between devices with their start and end apart: 5, of which 5 were waited for; matrix products, arithmetic and copies ran while one was open for 4% of the time, Pallas kernels for 0%

commit v1 on v0

v1 whole, which is shorter than its diff:
```python
import functools

import jax
import jax.numpy as jnp
from jax import lax
from jax.experimental import pallas as pl
from jax.experimental.pallas import tpu as pltpu
from jax.sharding import PartitionSpec as P

learn_rate = 0.1
epsilon = 1e-08

LANES = 128
TAG_ROWS = 8
DIGIT = 256
SLOT_BLOCK = 512
COPIES = 4


def pack_kernel(cap, deltas_ref, ids_ref, counts_ref, live_ref, out_ref):
    per = LANES // cap
    n_dest, _, width = out_ref.shape
    out_ref[:, 0:cap, :] = deltas_ref[...].reshape(n_dest, cap, width)
    sub = lax.broadcasted_iota(jnp.int32, (TAG_ROWS, LANES), 0)
    for r in range(n_dest // per):
        lanes = pl.ds(r * LANES, LANES)
        ids = ids_ref[lanes][None, :]
        weight = (counts_ref[lanes] * live_ref[lanes])[None, :]
        upper = lax.shift_right_logical(ids, 8)
        lower = jnp.bitwise_and(ids, DIGIT - 1)
        tag = jnp.where(sub == 0, upper, jnp.where(sub == 1, lower, jnp.where(sub == 2, weight, 0)))
        tag = tag.astype(jnp.float32).astype(jnp.bfloat16)
        out_ref[pl.ds(r * per, per), cap : cap + TAG_ROWS, :] = jnp.broadcast_to(
            tag[None], (per, TAG_ROWS, LANES)
        )


def copies(src, dst, sem):
    rows = src.shape[0] // COPIES
    return [
        pltpu.make_async_copy(
            src.at[pl.ds(i * rows, rows)], dst.at[pl.ds(i * rows, rows)], sem.at[i]
        )
        for i in range(COPIES)
    ]


def slots_kernel(
    cap, me_ref, got_ref, table_hbm, accum_hbm,
    reply_ref, new_t_ref, new_a_ref, ids_ref,
    tab, acc, id_row, id_smem, picked_t, picked_a, sem_t, sem_a, sem_i,
):
    loads = copies(table_hbm, tab, sem_t) + copies(accum_hbm, acc, sem_a)
    for load in loads:
        load.start()
    n_src, _, width = got_ref.shape
    n = n_src * cap
    per = LANES // cap
    first = lax.rem(me_ref[0], per) * cap
    lane = lax.broadcasted_iota(jnp.int32, (n_src, cap, LANES), 2)
    slot = lax.broadcasted_iota(jnp.int32, (n_src, cap, LANES), 1)
    mine = lane == slot + first
    tags = got_ref[:, cap : cap + TAG_ROWS, :].astype(jnp.float32)

    def spread(i):
        own = jnp.where(mine, tags[:, i : i + 1, :], 0.0)
        return own.reshape(n, LANES).astype(jnp.bfloat16)

    upper, lower, weight = spread(0), spread(1), spread(2)
    ones = jnp.ones((LANES, LANES), jnp.bfloat16)
    one_row = jnp.ones((8, LANES), jnp.bfloat16)
    f32 = jnp.float32

    def down(x):
        return jnp.dot(x, ones, preferred_element_type=f32)

    def across(x):
        return lax.dot_general(one_row, x, (((1,), (1,)), ((), ())), preferred_element_type=f32)

    row_f = across(upper) * DIGIT + across(lower)
    id_row[...] = row_f.astype(jnp.int32)
    ids_copy = pltpu.make_async_copy(id_row.at[pl.ds(0, 1)], id_smem, sem_i)
    ids_copy.start()
    column = down(upper) * DIGIT + down(lower)
    row_f, weight_row = row_f[0:1], across(weight)[0:1]
    deltas = got_ref[:, 0:cap, :].reshape(n, width)
    values = jnp.concatenate([deltas, jnp.ones((n, LANES), jnp.bfloat16)], axis=1)
    block = min(SLOT_BLOCK, n)
    sums = []
    for b in range(n // block):
        mark = jnp.concatenate([column[b * block : (b + 1) * block]] * (n // LANES), axis=1)
        weighted = jnp.where(mark == row_f, weight_row, 0.0).astype(jnp.bfloat16)
        sums.append(jnp.dot(weighted, values, preferred_element_type=f32))
    ids_copy.wait()
    for load in loads:
        load.wait()

    def pick(s, carry):
        v = id_smem[0, s]
        ids_ref[0, s] = v
        picked_t[pl.ds(s, 1), :] = tab[pl.ds(v, 1), :]
        picked_a[pl.ds(s, 1), :] = acc[pl.ds(v, 1), :]
        return carry

    lax.fori_loop(0, n, pick, 0, unroll=16)
    for b in range(n // block):
        part = pl.ds(b * block, block)
        grad = sums[b][:, 0:width] / jnp.maximum(sums[b][:, width : width + LANES], 1.0)
        next_a = picked_a[part] + grad * grad
        next_t = picked_t[part] - learn_rate * grad / (jnp.sqrt(next_a) + epsilon)
        new_a_ref[part] = next_a
        new_t_ref[part] = next_t
        reply_ref[part] = next_t.astype(jnp.bfloat16)


def write_kernel(
    ids_ref, new_t_ref, new_a_ref, table_hbm, accum_hbm, out_t, out_a,
    tab, acc, sem_t, sem_a,
):
    loads = copies(table_hbm, tab, sem_t) + copies(accum_hbm, acc, sem_a)
    for load in loads:
        load.start()
    for load in loads:
        load.wait()

    def put(s, carry):
        v = ids_ref[0, s]
        tab[pl.ds(v, 1), :] = new_t_ref[pl.ds(s, 1), :]
        acc[pl.ds(v, 1), :] = new_a_ref[pl.ds(s, 1), :]
        return carry

    lax.fori_loop(0, new_t_ref.shape[0], put, 0, unroll=16)
    stores = copies(tab, out_t, sem_t) + copies(acc, out_a, sem_a)
    for store in stores:
        store.start()
    for store in stores:
        store.wait()


def on_device(deltas, row_ids, sample_counts, live, table, accum):
    axes = ("aa", "ba")
    n_dest = lax.axis_size(axes)
    width = deltas.shape[1]
    n = deltas.shape[0]
    cap = n // n_dest
    vmem = pl.BlockSpec(memory_space=pltpu.VMEM)
    smem = pl.BlockSpec(memory_space=pltpu.SMEM)
    anywhere = pl.BlockSpec(memory_space=pl.ANY)
    f32 = jnp.float32
    payload = pl.pallas_call(
        functools.partial(pack_kernel, cap),
        out_shape=jax.ShapeDtypeStruct((n_dest, cap + TAG_ROWS, width), jnp.bfloat16),
        in_specs=[vmem] * 4,
        out_specs=vmem,
        name="pack",
    )(deltas, row_ids, sample_counts, live)
    got = lax.all_to_all(payload, axes, split_axis=0, concat_axis=0, tiled=True)
    me = lax.axis_index(axes).astype(jnp.int32).reshape(1)
    rows = jax.ShapeDtypeStruct((n, width), f32)
    held = [pltpu.VMEM(table.shape, f32), pltpu.VMEM(accum.shape, f32)]
    replies, new_t, new_a, ids = pl.pallas_call(
        functools.partial(slots_kernel, cap),
        out_shape=(
            jax.ShapeDtypeStruct((n, width), jnp.bfloat16), rows, rows,
            jax.ShapeDtypeStruct((1, n), jnp.int32),
        ),
        in_specs=[smem, vmem, anywhere, anywhere],
        out_specs=(vmem, vmem, vmem, smem),
        scratch_shapes=held + [
            pltpu.VMEM((8, n), jnp.int32), pltpu.SMEM((1, n), jnp.int32),
            pltpu.VMEM((n, width), f32), pltpu.VMEM((n, width), f32),
            pltpu.SemaphoreType.DMA((COPIES,)), pltpu.SemaphoreType.DMA((COPIES,)),
            pltpu.SemaphoreType.DMA,
        ],
        name="slots",
    )(me, got, table, accum)
    returned = lax.all_to_all(
        replies.reshape(n_dest, cap, width), axes, split_axis=0, concat_axis=0, tiled=True
    )
    new_table, new_accum = pl.pallas_call(
        write_kernel,
        out_shape=(
            jax.ShapeDtypeStruct(table.shape, f32), jax.ShapeDtypeStruct(accum.shape, f32),
        ),
        in_specs=[smem, vmem, vmem, anywhere, anywhere],
        out_specs=(anywhere, anywhere),
        scratch_shapes=held + [
            pltpu.SemaphoreType.DMA((COPIES,)), pltpu.SemaphoreType.DMA((COPIES,)),
        ],
        cost_estimate=pl.CostEstimate(flops=10**9, transcendentals=0, bytes_accessed=8 * 2**20),
        name="write",
    )(ids, new_t, new_a, table, accum)
    return (new_table, new_accum, returned.reshape(-1, width))


def solution(mesh):
    placed = (
        P(("aa", "ba"), None),
        P(("aa", "ba")),
        P(("aa", "ba")),
        P(("aa", "ba")),
        P(("aa", "ba"), None),
        P(("aa", "ba"), None),
    )
    return jax.shard_map(
        on_device,
        mesh=mesh,
        in_specs=placed,
        out_specs=(P(("aa", "ba"), None), P(("aa", "ba"), None), P(("aa", "ba"), None)),
        check_vma=False,
    )
```

time: 112 us -> 36.1 us (0.32)
  blocking collectives: 24.8 us -> 0 us
  matrix products: 24.7 us -> 0 us
  Pallas kernels: 0 us -> 12.6 us
  waiting for transfers between devices: 22.2 us -> 11.3 us
  starting transfers between devices: 19.6 us -> 9.95 us
  other arithmetic: 9 us -> 0 us
  local copies, waits for them, and re-layouts: 9.66 us -> 1.33 us
    all_to_all x3 -> x0, blocking collectives: 24.8 us -> none  [the longest x1 8.64 us: on_device(): lax.all_to_all(replies, 'aa', split_axis=0, concat_axis=0, tiled=True)]
    dot_general x24 -> x0, matrix products: 24.7 us -> none  [the longest x8 18.9 us: owner_block(): lax.dot_general(weighted.astype(jnp.bfloat16), slot_rows, contract, prefe...]
    pallas_call x0 -> x3, Pallas kernels: none -> 12.6 us  [the longest x1 5.89 us: on_device(): pl.pallas_call(write_kernel, out_shape=(jax.ShapeDtypeStruct(table.shape,...]
    all_to_all x5 -> x2, waiting for transfers between devices: 22.2 us -> 11.3 us  [the longest x1 8.94 us: on_device(): got = lax.all_to_all(payload, axes, split_axis=0, concat_axis=0, tiled=True)]
    all_to_all x5 -> x2, starting transfers between devices: 19.6 us -> 9.95 us  [the longest x1 7.33 us: on_device(): got = lax.all_to_all(payload, axes, split_axis=0, concat_axis=0, tiled=True)]
    add x8 -> x0, other arithmetic: 5.17 us -> none  [owner_block(): matched = local[:, None] == (start + within)[None, :]]
    dynamic_slice x8 -> x0, local copies, waits for them, and re-layouts: 4.69 us -> none  [on_device(): lax.scan(owner_block, start_replies, (offsets, table_blocks, accum_blocks))]
    all_to_all x7 -> x0, local copies, waits for them, and re-layouts: 2.48 us -> none  [the longest x1 0.67 us: on_device(): lax.all_to_all(payload[0], 'aa', split_axis=0, concat_axis=0, tiled=True)]
  transfers between devices with their start and end apart: 5 -> 2, of which waited for: 5 -> 2; matrix products, arithmetic and copies ran while one was open for 4% -> 0% of each run, Pallas kernels for 0% -> 16%
where the time goes in v1:
time: 36.1 us; the launch traced here: 35.8 us
  Pallas kernels  12.6 us (35%)
  waiting for transfers between devices  11.3 us (31%)
  starting transfers between devices  9.95 us (28%)
  local copies, waits for them, and re-layouts  1.33 us (4%)
  between operations  0.67 us (2%)
    all_to_all x1, waiting for transfers between devices, on_device(): got = lax.all_to_all(payload, axes, split_axis=0, concat_axis=0, tiled=True)  8.94 us
    all_to_all x1, starting transfers between devices, on_device(): got = lax.all_to_all(payload, axes, split_axis=0, concat_axis=0, tiled=True)  7.33 us
    pallas_call x1, Pallas kernels, on_device(): pl.pallas_call(write_kernel, out_shape=(jax.ShapeDtypeStruct(table.shape,...  5.89 us
    pallas_call x1, Pallas kernels, on_device(): pl.pallas_call(functools.partial(slots_kernel, cap), out_shape=(jax.Shape...  5.1 us
    all_to_all x1, starting transfers between devices, on_device(): lax.all_to_all(replies.reshape(n_dest, cap, width), axes, split_axis=0, c...  2.62 us
    all_to_all x1, waiting for transfers between devices, on_device(): lax.all_to_all(replies.reshape(n_dest, cap, width), axes, split_axis=0, c...  2.31 us
    pallas_call x1, Pallas kernels, on_device(): pl.pallas_call(functools.partial(pack_kernel, cap), out_shape=jax.ShapeDt...  1.63 us
    unnamed x3, local copies, waits for them, and re-layouts  1.33 us
  transfers between devices with their start and end apart: 2, of which 2 were waited for; matrix products, arithmetic and copies ran while one was open for 0% of the time, Pallas kernels for 16%

profile of v1, /device:TPU:0, one launch (start us, length us, event | category | flops | bytes accessed | tf_op | source)
XLA Modules:
  0.0 35.8 jit_solution(9859477806247859026)
XLA Ops:
  0.6 1.6 %pack.1 = bf16[32,24,128]{2,1,0:T(8,128)(2,1)} custom-call(bf16[512,128]{1,0:T(8,128)(2,1)} %deltas_ref.1, s32[512]{0:T(512)} %ids_ref.1, s32[512]{0:T(512)} %counts_ref.1, s32[512]{0:T(512)} %live_ref.1), custom_call_target="tpu_custom_call" | custom-call | tf_op jit(solution)/shard_map/pack/pallas_call | solution.py:150
  2.3 7.3 %all-to-all-start = ((bf16[32,24,128]{2,1,0:T(8,128)(2,1)}), bf16[32,24,128]{2,1,0:T(8,128)(2,1)S(1)}, u32[]{:S(2)}, u32[]{:S(2)}) async-start(bf16[32,24,128]{2,1,0:T(8,128)(2,1)} %pack.1), calls=%async_computation | async-start | bytes 393216 | tf_op jit(solution)/shard_map/all_to_all | solution.py:157
  9.6 8.9 %all-to-all-done.got_ref = bf16[32,24,128]{2,1,0:T(8,128)(2,1)S(1)} async-done(((bf16[32,24,128]{2,1,0:T(8,128)(2,1)}), bf16[32,24,128]{2,1,0:T(8,128)(2,1)S(1)}, u32[]{:S(2)}, u32[]{:S(2)}) %all-to-all-start) | async-done | bytes 196640 | tf_op jit(solution)/shard_map/all_to_all | solution.py:157
  18.5 0.0 copy-start
  18.5 0.7 %copy-done = bf16[32,24,128]{2,1,0:T(8,128)(2,1)} copy-done((bf16[32,24,128]{2,1,0:T(8,128)(2,1)}, bf16[32,24,128]{2,1,0:T(8,128)(2,1)S(1)}, u32[]{:S(2)}) %copy-start) | copy-done | bytes 196632
  19.2 5.1 %slots.1 = (bf16[512,128]{1,0:T(8,128)(2,1)}, f32[512,128]{1,0:T(8,128)}, f32[512,128]{1,0:T(8,128)}, s32[1,512]{1,0:T(1,128)}) custom-call(s32[1]{0:T(128)} %bitcast.me_ref, bf16[32,24,128]{2,1,0:T(8,128)(2,1)} %copy-done, f32[4096,128]{1,0:T(8,128)} %table_hbm.3, f32[4096,128]{1,0:T(8,128)} %accum_hbm.3), custom_call_target="tpu_custom_call" | custom-call | tf_op jit(solution)/shard_map/slots/pallas_call | solution.py:161
  24.3 2.6 %all-to-all-start.1 = ((bf16[32,16,128]{2,1,0:T(8,128)(2,1)}), bf16[32,16,128]{2,1,0:T(8,128)(2,1)S(1)}, u32[]{:S(2)}, u32[]{:S(2)}) async-start(bf16[32,16,128]{2,1,0:T(8,128)(2,1)} %bitcast.4), calls=%async_computation.1 | async-start | bytes 262144 | tf_op jit(solution)/shard_map/all_to_all | solution.py:177
  27.0 5.9 %write.1 = (f32[4096,128]{1,0:T(8,128)}, f32[4096,128]{1,0:T(8,128)}) custom-call(s32[1,512]{1,0:T(1,128)} %get-tuple-element.9.ids_ref, f32[512,128]{1,0:T(8,128)} %get-tuple-element.10.new_t_ref, f32[512,128]{1,0:T(8,128)} %get-tuple-element.11.new_a_ref, f32[4096,128]{1,0:T(8,128)} %table_hbm.3, f32[4096,128]{1,0:T(8,128)} %accum_hbm.3), custom_call_target="tpu_custom_call" | custom-call | flops 1000000000 | bytes 8388608 | tf_op jit(solution)/shard_map/write/pallas_call | solution.py:180
  32.9 2.3 %all-to-all-done.1 = bf16[32,16,128]{2,1,0:T(8,128)(2,1)S(1)} async-done(((bf16[32,16,128]{2,1,0:T(8,128)(2,1)}), bf16[32,16,128]{2,1,0:T(8,128)(2,1)S(1)}, u32[]{:S(2)}, u32[]{:S(2)}) %all-to-all-start.1) | async-done | bytes 131104 | tf_op jit(solution)/shard_map/all_to_all | solution.py:177
  35.2 0.7 %copy.10 = bf16[512,128]{1,0:T(8,128)(2,1)} copy(bf16[512,128]{1,0:T(8,128)(2,1)S(1)} %bitcast.3) | data formatting | bytes 262144
Async XLA Ops:
  2.3 16.3 %all-to-all-start = ((bf16[32,24,128]{2,1,0:T(8,128)(2,1)}), bf16[32,24,128]{2,1,0:T(8,128)(2,1)S(1)}, u32[]{:S(2)}, u32[]{:S(2)}) async-start(bf16[32,24,128]{2,1,0:T(8,128)(2,1)} %pack.1), calls=%async_computation | async-start | bytes 393216 | tf_op jit(solution)/shard_map/all_to_all | solution.py:157
  18.5 0.7 %copy-start = (bf16[32,24,128]{2,1,0:T(8,128)(2,1)}, bf16[32,24,128]{2,1,0:T(8,128)(2,1)S(1)}, u32[]{:S(2)}) copy-start(bf16[32,24,128]{2,1,0:T(8,128)(2,1)S(1)} %all-to-all-done.got_ref) | copy-start | bytes 589828
  24.3 10.8 %all-to-all-start.1 = ((bf16[32,16,128]{2,1,0:T(8,128)(2,1)}), bf16[32,16,128]{2,1,0:T(8,128)(2,1)S(1)}, u32[]{:S(2)}, u32[]{:S(2)}) async-start(bf16[32,16,128]{2,1,0:T(8,128)(2,1)} %bitcast.4), calls=%async_computation.1 | async-start | bytes 262144 | tf_op jit(solution)/shard_map/all_to_all | solution.py:177

commit v2 on v1

--- a/solution.py
+++ b/solution.py
@@ -15,12 +15,25 @@
 DIGIT = 256
 SLOT_BLOCK = 512
 COPIES = 4
-
-
-def pack_kernel(cap, deltas_ref, ids_ref, counts_ref, live_ref, out_ref):
+MIB = 2**20
+PACK_VMEM = 8 * MIB
+
+
+def pack_kernel(
+    cap, deltas_hbm, ids_hbm, counts_hbm, live_hbm, out_ref, ids_ref, counts_ref, live_ref, sem
+):
     per = LANES // cap
-    n_dest, _, width = out_ref.shape
-    out_ref[:, 0:cap, :] = deltas_ref[...].reshape(n_dest, cap, width)
+    n_dest = out_ref.shape[0]
+    loads = [
+        pltpu.make_async_copy(ids_hbm, ids_ref, sem.at[0]),
+        pltpu.make_async_copy(counts_hbm, counts_ref, sem.at[1]),
+        pltpu.make_async_copy(live_hbm, live_ref, sem.at[2]),
+        pltpu.make_async_copy(deltas_hbm, out_ref.at[:, pl.ds(0, cap), :], sem.at[3]),
+    ]
+    for load in loads:
+        load.start()
+    for load in loads[:3]:
+        load.wait()
     sub = lax.broadcasted_iota(jnp.int32, (TAG_ROWS, LANES), 0)
     for r in range(n_dest // per):
         lanes = pl.ds(r * LANES, LANES)
@@ -33,6 +46,7 @@
         out_ref[pl.ds(r * per, per), cap : cap + TAG_ROWS, :] = jnp.broadcast_to(
             tag[None], (per, TAG_ROWS, LANES)
         )
+    loads[3].wait()
 
 
 def copies(src, dst, sem):
@@ -46,7 +60,7 @@
 
 
 def slots_kernel(
-    cap, me_ref, got_ref, table_hbm, accum_hbm,
+    cap, axes, got_ref, table_hbm, accum_hbm,
     reply_ref, new_t_ref, new_a_ref, ids_ref,
     tab, acc, id_row, id_smem, picked_t, picked_a, sem_t, sem_a, sem_i,
 ):
@@ -56,7 +70,7 @@
     n_src, _, width = got_ref.shape
     n = n_src * cap
     per = LANES // cap
-    first = lax.rem(me_ref[0], per) * cap
+    first = lax.rem(lax.axis_index(axes), per) * cap
     lane = lax.broadcasted_iota(jnp.int32, (n_src, cap, LANES), 2)
     slot = lax.broadcasted_iota(jnp.int32, (n_src, cap, LANES), 1)
     mine = lane == slot + first
@@ -137,6 +151,10 @@
         store.wait()
 
 
+def in_hbm(*arrays):
+    return [pltpu.with_memory_space_constraint(x, pltpu.HBM) for x in arrays]
+
+
 def on_device(deltas, row_ids, sample_counts, live, table, accum):
     axes = ("aa", "ba")
     n_dest = lax.axis_size(axes)
@@ -145,26 +163,29 @@
     cap = n // n_dest
     vmem = pl.BlockSpec(memory_space=pltpu.VMEM)
     smem = pl.BlockSpec(memory_space=pltpu.SMEM)
-    anywhere = pl.BlockSpec(memory_space=pl.ANY)
+    hbm = pl.BlockSpec(memory_space=pltpu.HBM)
     f32 = jnp.float32
+    slots_vmem = 16 * MIB if n <= SLOT_BLOCK else 60 * MIB
+    write_vmem = 16 * MIB
     payload = pl.pallas_call(
         functools.partial(pack_kernel, cap),
         out_shape=jax.ShapeDtypeStruct((n_dest, cap + TAG_ROWS, width), jnp.bfloat16),
-        in_specs=[vmem] * 4,
+        in_specs=[hbm] * 4,
         out_specs=vmem,
+        scratch_shapes=[pltpu.VMEM((n,), jnp.int32)] * 3 + [pltpu.SemaphoreType.DMA((4,))],
+        compiler_params=pltpu.CompilerParams(vmem_limit_bytes=PACK_VMEM),
         name="pack",
-    )(deltas, row_ids, sample_counts, live)
+    )(*in_hbm(deltas.reshape(n_dest, cap, width), row_ids, sample_counts, live))
     got = lax.all_to_all(payload, axes, split_axis=0, concat_axis=0, tiled=True)
-    me = lax.axis_index(axes).astype(jnp.int32).reshape(1)
     rows = jax.ShapeDtypeStruct((n, width), f32)
     held = [pltpu.VMEM(table.shape, f32), pltpu.VMEM(accum.shape, f32)]
     replies, new_t, new_a, ids = pl.pallas_call(
-        functools.partial(slots_kernel, cap),
+        functools.partial(slots_kernel, cap, axes),
         out_shape=(
             jax.ShapeDtypeStruct((n, width), jnp.bfloat16), rows, rows,
             jax.ShapeDtypeStruct((1, n), jnp.int32),
         ),
-        in_specs=[smem, vmem, anywhere, anywhere],
+        in_specs=[vmem, hbm, hbm],
         out_specs=(vmem, vmem, vmem, smem),
         scratch_shapes=held + [
             pltpu.VMEM((8, n), jnp.int32), pltpu.SMEM((1, n), jnp.int32),
@@ -172,8 +193,9 @@
             pltpu.SemaphoreType.DMA((COPIES,)), pltpu.SemaphoreType.DMA((COPIES,)),
             pltpu.SemaphoreType.DMA,
         ],
+        compiler_params=pltpu.CompilerParams(vmem_limit_bytes=slots_vmem),
         name="slots",
-    )(me, got, table, accum)
+    )(got, *in_hbm(table, accum))
     returned = lax.all_to_all(
         replies.reshape(n_dest, cap, width), axes, split_axis=0, concat_axis=0, tiled=True
     )
@@ -182,14 +204,15 @@
         out_shape=(
             jax.ShapeDtypeStruct(table.shape, f32), jax.ShapeDtypeStruct(accum.shape, f32),
         ),
-        in_specs=[smem, vmem, vmem, anywhere, anywhere],
-        out_specs=(anywhere, anywhere),
+        in_specs=[smem, vmem, vmem, hbm, hbm],
+        out_specs=(hbm, hbm),
         scratch_shapes=held + [
             pltpu.SemaphoreType.DMA((COPIES,)), pltpu.SemaphoreType.DMA((COPIES,)),
         ],
         cost_estimate=pl.CostEstimate(flops=10**9, transcendentals=0, bytes_accessed=8 * 2**20),
+        compiler_params=pltpu.CompilerParams(vmem_limit_bytes=write_vmem),
         name="write",
-    )(ids, new_t, new_a, table, accum)
+    )(ids, new_t, new_a, *in_hbm(table, accum))
     return (new_table, new_accum, returned.reshape(-1, width))
 
 

time: 36.1 us -> 33.5 us (0.928)
  blocking collectives: 0 us -> 16.1 us
  waiting for transfers between devices: 11.3 us -> 2.78 us
  starting transfers between devices: 9.95 us -> 2.62 us
  Pallas kernels: 12.6 us -> 10.5 us
  local copies, waits for them, and re-layouts: 1.33 us -> 0.66 us
    all_to_all x0 -> x1, blocking collectives: none -> 16.1 us  [on_device(): got = lax.all_to_all(payload, axes, split_axis=0, concat_axis=0, tiled=True)]
    all_to_all x1 -> x0, waiting for transfers between devices: 8.94 us -> none  [on_device(): got = lax.all_to_all(payload, axes, split_axis=0, concat_axis=0, tiled=True)]
    all_to_all x1 -> x0, starting transfers between devices: 7.33 us -> none  [on_device(): got = lax.all_to_all(payload, axes, split_axis=0, concat_axis=0, tiled=True)]
    pallas_call x1, Pallas kernels: 5.1 us -> 4.06 us  [on_device(): pl.pallas_call(functools.partial(slots_kernel, cap, axes), out_shape=(jax...]
    unnamed x3 -> x1, local copies, waits for them, and re-layouts: 1.33 us -> 0.66 us
    pallas_call x1, Pallas kernels: 1.63 us -> 0.99 us  [on_device(): pl.pallas_call(functools.partial(pack_kernel, cap), out_shape=jax.ShapeDt...]
    all_to_all x1, waiting for transfers between devices: 2.31 us -> 2.78 us  [on_device(): lax.all_to_all(replies.reshape(n_dest, cap, width), axes, split_axis=0, c...]
    pallas_call x1, Pallas kernels: 5.89 us -> 5.41 us  [on_device(): pl.pallas_call(write_kernel, out_shape=(jax.ShapeDtypeStruct(table.shape,...]
  transfers between devices with their start and end apart: 2 -> 1, of which waited for: 2 -> 1; matrix products, arithmetic and copies ran while one was open for 0% -> 0% of each run, Pallas kernels for 16% -> 16%
where the time goes in v2:
time: 33.5 us; the launch traced here: 33.3 us
  blocking collectives  16.1 us (48%)
  Pallas kernels  10.5 us (31%)
  waiting for transfers between devices  2.78 us (8%)
  starting transfers between devices  2.62 us (8%)
  local copies, waits for them, and re-layouts  0.66 us (2%)
  between operations  0.66 us (2%)
    all_to_all x1, blocking collectives, on_device(): got = lax.all_to_all(payload, axes, split_axis=0, concat_axis=0, tiled=True)  16.1 us
    pallas_call x1, Pallas kernels, on_device(): pl.pallas_call(write_kernel, out_shape=(jax.ShapeDtypeStruct(table.shape,...  5.41 us
    pallas_call x1, Pallas kernels, on_device(): pl.pallas_call(functools.partial(slots_kernel, cap, axes), out_shape=(jax...  4.06 us
    all_to_all x1, waiting for transfers between devices, on_device(): lax.all_to_all(replies.reshape(n_dest, cap, width), axes, split_axis=0, c...  2.78 us
    all_to_all x1, starting transfers between devices, on_device(): lax.all_to_all(replies.reshape(n_dest, cap, width), axes, split_axis=0, c...  2.62 us
    pallas_call x1, Pallas kernels, on_device(): pl.pallas_call(functools.partial(pack_kernel, cap), out_shape=jax.ShapeDt...  0.99 us
  transfers between devices with their start and end apart: 1, of which 1 were waited for; matrix products, arithmetic and copies ran while one was open for 0% of the time, Pallas kernels for 16%

profile of v2, /device:TPU:0, one launch (start us, length us, event | category | flops | bytes accessed | tf_op | source)
XLA Modules:
  0.0 33.3 jit_solution(14411108768685961123)
XLA Ops:
  0.6 1.0 %pack.1 = bf16[32,24,128]{2,1,0:T(8,128)(2,1)S(1)} custom-call(bf16[32,16,128]{2,1,0:T(8,128)(2,1)} %bitcast.4, s32[512]{0:T(512)} %ids_hbm.1, s32[512]{0:T(512)} %counts_hbm.1, s32[512]{0:T(512)} %live_hbm.1), custom_call_target="tpu_custom_call" | custom-call | tf_op jit(solution)/shard_map/pack/pallas_call | solution.py:170
  1.6 16.1 %all_to_all.10.got_ref = bf16[32,24,128]{2,1,0:T(8,128)(2,1)S(1)} all-to-all(bf16[32,24,128]{2,1,0:T(8,128)(2,1)S(1)} %pack.1), channel_id=1, replica_groups=mesh['aa'=4,'ba'=8] {'aa','ba'}, dimensions={0} | all-to-all | bytes 393216 | tf_op jit(solution)/shard_map/all_to_all | solution.py:179
  17.7 4.1 %slots.1 = (bf16[512,128]{1,0:T(8,128)(2,1)}, f32[512,128]{1,0:T(8,128)S(1)}, f32[512,128]{1,0:T(8,128)S(1)}, s32[1,512]{1,0:T(1,128)S(1)}) custom-call(bf16[32,24,128]{2,1,0:T(8,128)(2,1)S(1)} %all_to_all.10.got_ref, f32[4096,128]{1,0:T(8,128)} %table_hbm.3, f32[4096,128]{1,0:T(8,128)} %accum_hbm.3), custom_call_target="tpu_custom_call" | custom-call | tf_op jit(solution)/shard_map/slots/pallas_call | solution.py:182
  21.8 2.6 %all-to-all-start.1 = ((bf16[32,16,128]{2,1,0:T(8,128)(2,1)}), bf16[32,16,128]{2,1,0:T(8,128)(2,1)S(1)}, u32[]{:S(2)}, u32[]{:S(2)}) async-start(bf16[32,16,128]{2,1,0:T(8,128)(2,1)} %bitcast.1), calls=%async_computation.1 | async-start | bytes 262144 | tf_op jit(solution)/shard_map/all_to_all | solution.py:199
  24.4 5.4 %write.1 = (f32[4096,128]{1,0:T(8,128)}, f32[4096,128]{1,0:T(8,128)}) custom-call(s32[1,512]{1,0:T(1,128)S(1)} %get-tuple-element.9.ids_ref, f32[512,128]{1,0:T(8,128)S(1)} %get-tuple-element.10.new_t_ref, f32[512,128]{1,0:T(8,128)S(1)} %get-tuple-element.11.new_a_ref, f32[4096,128]{1,0:T(8,128)} %table_hbm.3, f32[4096,128]{1,0:T(8,128)} %accum_hbm.3), custom_call_target="tpu_custom_call" | custom-call | flops 1000000000 | bytes 8388608 | tf_op jit(solution)/shard_map/write/pallas_call | solution.py:202
  29.8 2.8 %all-to-all-done.1 = bf16[32,16,128]{2,1,0:T(8,128)(2,1)S(1)} async-done(((bf16[32,16,128]{2,1,0:T(8,128)(2,1)}), bf16[32,16,128]{2,1,0:T(8,128)(2,1)S(1)}, u32[]{:S(2)}, u32[]{:S(2)}) %all-to-all-start.1) | async-done | bytes 131104 | tf_op jit(solution)/shard_map/all_to_all | solution.py:199
  32.6 0.7 %copy.10 = bf16[512,128]{1,0:T(8,128)(2,1)} copy(bf16[512,128]{1,0:T(8,128)(2,1)S(1)} %bitcast.3) | data formatting | bytes 262144
Async XLA Ops:
  21.8 10.8 %all-to-all-start.1 = ((bf16[32,16,128]{2,1,0:T(8,128)(2,1)}), bf16[32,16,128]{2,1,0:T(8,128)(2,1)S(1)}, u32[]{:S(2)}, u32[]{:S(2)}) async-start(bf16[32,16,128]{2,1,0:T(8,128)(2,1)} %bitcast.1), calls=%async_computation.1 | async-start | bytes 262144 | tf_op jit(solution)/shard_map/all_to_all | solution.py:199

commit v3 on v2

--- a/solution.py
+++ b/solution.py
@@ -60,13 +60,9 @@
 
 
 def slots_kernel(
-    cap, axes, got_ref, table_hbm, accum_hbm,
-    reply_ref, new_t_ref, new_a_ref, ids_ref,
-    tab, acc, id_row, id_smem, picked_t, picked_a, sem_t, sem_a, sem_i,
+    cap, axes, got_ref, table_ref, accum_ref, reply_ref, new_t_ref, new_a_ref, ids_ref,
+    id_smem, picked_t, picked_a, sem_i,
 ):
-    loads = copies(table_hbm, tab, sem_t) + copies(accum_hbm, acc, sem_a)
-    for load in loads:
-        load.start()
     n_src, _, width = got_ref.shape
     n = n_src * cap
     per = LANES // cap
@@ -92,8 +88,8 @@
         return lax.dot_general(one_row, x, (((1,), (1,)), ((), ())), preferred_element_type=f32)
 
     row_f = across(upper) * DIGIT + across(lower)
-    id_row[...] = row_f.astype(jnp.int32)
-    ids_copy = pltpu.make_async_copy(id_row.at[pl.ds(0, 1)], id_smem, sem_i)
+    ids_ref[...] = row_f.astype(jnp.int32)
+    ids_copy = pltpu.make_async_copy(ids_ref.at[pl.ds(0, 1)], id_smem, sem_i)
     ids_copy.start()
     column = down(upper) * DIGIT + down(lower)
     row_f, weight_row = row_f[0:1], across(weight)[0:1]
@@ -106,17 +102,17 @@
         weighted = jnp.where(mark == row_f, weight_row, 0.0).astype(jnp.bfloat16)
         sums.append(jnp.dot(weighted, values, preferred_element_type=f32))
     ids_copy.wait()
-    for load in loads:
-        load.wait()
-
-    def pick(s, carry):
-        v = id_smem[0, s]
-        ids_ref[0, s] = v
-        picked_t[pl.ds(s, 1), :] = tab[pl.ds(v, 1), :]
-        picked_a[pl.ds(s, 1), :] = acc[pl.ds(v, 1), :]
-        return carry
-
-    lax.fori_loop(0, n, pick, 0, unroll=16)
+
+    def pick_t(s, carry):
+        picked_t[pl.ds(s, 1), :] = table_ref[pl.ds(id_smem[0, s], 1), :]
+        return carry
+
+    def pick_a(s, carry):
+        picked_a[pl.ds(s, 1), :] = accum_ref[pl.ds(id_smem[0, s], 1), :]
+        return carry
+
+    lax.fori_loop(0, n, pick_t, 0, unroll=32)
+    lax.fori_loop(0, n, pick_a, 0, unroll=32)
     for b in range(n // block):
         part = pl.ds(b * block, block)
         grad = sums[b][:, 0:width] / jnp.maximum(sums[b][:, width : width + LANES], 1.0)
@@ -129,21 +125,27 @@
 
 def write_kernel(
     ids_ref, new_t_ref, new_a_ref, table_hbm, accum_hbm, out_t, out_a,
-    tab, acc, sem_t, sem_a,
+    id_smem, tab, acc, sem_t, sem_a, sem_i,
 ):
     loads = copies(table_hbm, tab, sem_t) + copies(accum_hbm, acc, sem_a)
     for load in loads:
         load.start()
+    ids_copy = pltpu.make_async_copy(ids_ref.at[pl.ds(0, 1)], id_smem, sem_i)
+    ids_copy.start()
+    ids_copy.wait()
     for load in loads:
         load.wait()
 
-    def put(s, carry):
-        v = ids_ref[0, s]
-        tab[pl.ds(v, 1), :] = new_t_ref[pl.ds(s, 1), :]
-        acc[pl.ds(v, 1), :] = new_a_ref[pl.ds(s, 1), :]
-        return carry
-
-    lax.fori_loop(0, new_t_ref.shape[0], put, 0, unroll=16)
+    def put_t(s, carry):
+        tab[pl.ds(id_smem[0, s], 1), :] = new_t_ref[pl.ds(s, 1), :]
+        return carry
+
+    def put_a(s, carry):
+        acc[pl.ds(id_smem[0, s], 1), :] = new_a_ref[pl.ds(s, 1), :]
+        return carry
+
+    lax.fori_loop(0, new_t_ref.shape[0], put_t, 0, unroll=32)
+    lax.fori_loop(0, new_t_ref.shape[0], put_a, 0, unroll=32)
     stores = copies(tab, out_t, sem_t) + copies(acc, out_a, sem_a)
     for store in stores:
         store.start()
@@ -162,7 +164,6 @@
     n = deltas.shape[0]
     cap = n // n_dest
     vmem = pl.BlockSpec(memory_space=pltpu.VMEM)
-    smem = pl.BlockSpec(memory_space=pltpu.SMEM)
     hbm = pl.BlockSpec(memory_space=pltpu.HBM)
     f32 = jnp.float32
     slots_vmem = 16 * MIB if n <= SLOT_BLOCK else 60 * MIB
@@ -174,6 +175,7 @@
         out_specs=vmem,
         scratch_shapes=[pltpu.VMEM((n,), jnp.int32)] * 3 + [pltpu.SemaphoreType.DMA((4,))],
         compiler_params=pltpu.CompilerParams(vmem_limit_bytes=PACK_VMEM),
+        cost_estimate=pl.CostEstimate(flops=10**10, transcendentals=0, bytes_accessed=2**24),
         name="pack",
     )(*in_hbm(deltas.reshape(n_dest, cap, width), row_ids, sample_counts, live))
     got = lax.all_to_all(payload, axes, split_axis=0, concat_axis=0, tiled=True)
@@ -183,19 +185,17 @@
         functools.partial(slots_kernel, cap, axes),
         out_shape=(
             jax.ShapeDtypeStruct((n, width), jnp.bfloat16), rows, rows,
-            jax.ShapeDtypeStruct((1, n), jnp.int32),
+            jax.ShapeDtypeStruct((8, n), jnp.int32),
         ),
-        in_specs=[vmem, hbm, hbm],
-        out_specs=(vmem, vmem, vmem, smem),
-        scratch_shapes=held + [
-            pltpu.VMEM((8, n), jnp.int32), pltpu.SMEM((1, n), jnp.int32),
-            pltpu.VMEM((n, width), f32), pltpu.VMEM((n, width), f32),
-            pltpu.SemaphoreType.DMA((COPIES,)), pltpu.SemaphoreType.DMA((COPIES,)),
-            pltpu.SemaphoreType.DMA,
+        in_specs=[vmem] * 3,
+        out_specs=(vmem,) * 4,
+        scratch_shapes=[
+            pltpu.SMEM((1, n), jnp.int32), pltpu.VMEM((n, width), f32),
+            pltpu.VMEM((n, width), f32), pltpu.SemaphoreType.DMA,
         ],
         compiler_params=pltpu.CompilerParams(vmem_limit_bytes=slots_vmem),
         name="slots",
-    )(got, *in_hbm(table, accum))
+    )(got, table, accum)
     returned = lax.all_to_all(
         replies.reshape(n_dest, cap, width), axes, split_axis=0, concat_axis=0, tiled=True
     )
@@ -204,10 +204,11 @@
         out_shape=(
             jax.ShapeDtypeStruct(table.shape, f32), jax.ShapeDtypeStruct(accum.shape, f32),
         ),
-        in_specs=[smem, vmem, vmem, hbm, hbm],
+        in_specs=[vmem, vmem, vmem, hbm, hbm],
         out_specs=(hbm, hbm),
-        scratch_shapes=held + [
+        scratch_shapes=[pltpu.SMEM((1, n), jnp.int32)] + held + [
             pltpu.SemaphoreType.DMA((COPIES,)), pltpu.SemaphoreType.DMA((COPIES,)),
+            pltpu.SemaphoreType.DMA,
         ],
         cost_estimate=pl.CostEstimate(flops=10**9, transcendentals=0, bytes_accessed=8 * 2**20),
         compiler_params=pltpu.CompilerParams(vmem_limit_bytes=write_vmem),

time: 33.5 us -> 32.2 us (0.961)
  Pallas kernels: 10.5 us -> 8.86 us
    pallas_call x1, Pallas kernels: 4.06 us -> 2.55 us  [on_device(): pl.pallas_call(functools.partial(slots_kernel, cap, axes), out_shape=(jax...]
where the time goes in v3:
time: 32.2 us; the launch traced here: 31.9 us
  blocking collectives  16.1 us (50%)
  Pallas kernels  8.86 us (28%)
  waiting for transfers between devices  3.02 us (9%)
  starting transfers between devices  2.63 us (8%)
  between operations  0.68 us (2%)
  local copies, waits for them, and re-layouts  0.67 us (2%)
    all_to_all x1, blocking collectives, on_device(): got = lax.all_to_all(payload, axes, split_axis=0, concat_axis=0, tiled=True)  16.1 us
    pallas_call x1, Pallas kernels, on_device(): pl.pallas_call(write_kernel, out_shape=(jax.ShapeDtypeStruct(table.shape,...  5.18 us
    all_to_all x1, waiting for transfers between devices, on_device(): lax.all_to_all(replies.reshape(n_dest, cap, width), axes, split_axis=0, c...  3.02 us
    all_to_all x1, starting transfers between devices, on_device(): lax.all_to_all(replies.reshape(n_dest, cap, width), axes, split_axis=0, c...  2.63 us
    pallas_call x1, Pallas kernels, on_device(): pl.pallas_call(functools.partial(slots_kernel, cap, axes), out_shape=(jax...  2.55 us
    pallas_call x1, Pallas kernels, on_device(): pl.pallas_call(functools.partial(pack_kernel, cap), out_shape=jax.ShapeDt...  1.14 us
    unnamed x5, local copies, waits for them, and re-layouts  0.67 us
  transfers between devices with their start and end apart: 1, of which 1 were waited for; matrix products, arithmetic and copies ran while one was open for 0% of the time, Pallas kernels for 16%

profile of v3, /device:TPU:0, one launch (start us, length us, event | category | flops | bytes accessed | tf_op | source)
XLA Modules:
  0.0 31.9 jit_solution(17429686355597653845)
XLA Ops:
  0.6 0.0 copy-start
  0.6 0.0 copy-start.1
  0.7 1.1 %pack.1 = bf16[32,24,128]{2,1,0:T(8,128)(2,1)S(1)} custom-call(bf16[32,16,128]{2,1,0:T(8,128)(2,1)} %bitcast.4, s32[512]{0:T(512)} %ids_hbm.1, s32[512]{0:T(512)} %counts_hbm.1, s32[512]{0:T(512)} %live_hbm.1), custom_call_target="tpu_custom_call" | custom-call | flops 10000000000 | bytes 16777216 | tf_op jit(solution)/shard_map/pack/pallas_call | solution.py:171
  1.8 16.1 %all_to_all.10.got_ref = bf16[32,24,128]{2,1,0:T(8,128)(2,1)S(1)} all-to-all(bf16[32,24,128]{2,1,0:T(8,128)(2,1)S(1)} %pack.1), channel_id=1, replica_groups=mesh['aa'=4,'ba'=8] {'aa','ba'}, dimensions={0} | all-to-all | bytes 393216 | tf_op jit(solution)/shard_map/all_to_all | solution.py:181
  17.9 0.0 copy-done
  17.9 0.0 copy-done.1
  17.9 2.5 %slots.1 = (bf16[512,128]{1,0:T(8,128)(2,1)}, f32[512,128]{1,0:T(8,128)S(1)}, f32[512,128]{1,0:T(8,128)S(1)}, s32[8,512]{1,0:T(8,128)S(1)}) custom-call(bf16[32,24,128]{2,1,0:T(8,128)(2,1)S(1)} %all_to_all.10.got_ref, f32[4096,128]{1,0:T(8,128)S(1)} %copy-done, f32[4096,128]{1,0:T(8,128)S(1)} %copy-done.1), custom_call_target="tpu_custom_call" | custom-call | tf_op jit(solution)/shard_map/slots/pallas_call | solution.py:184
  20.4 2.6 %all-to-all-start.1 = ((bf16[32,16,128]{2,1,0:T(8,128)(2,1)}), bf16[32,16,128]{2,1,0:T(8,128)(2,1)S(1)}, u32[]{:S(2)}, u32[]{:S(2)}) async-start(bf16[32,16,128]{2,1,0:T(8,128)(2,1)} %bitcast.1), calls=%async_computation.1 | async-start | bytes 262144 | tf_op jit(solution)/shard_map/all_to_all | solution.py:199
  23.1 5.2 %write.1 = (f32[4096,128]{1,0:T(8,128)}, f32[4096,128]{1,0:T(8,128)}) custom-call(s32[8,512]{1,0:T(8,128)S(1)} %get-tuple-element.9.ids_ref, f32[512,128]{1,0:T(8,128)S(1)} %get-tuple-element.10.new_t_ref, f32[512,128]{1,0:T(8,128)S(1)} %get-tuple-element.11.new_a_ref, f32[4096,128]{1,0:T(8,128)} %table_hbm.1, f32[4096,128]{1,0:T(8,128)} %accum_hbm.1), custom_call_target="tpu_custom_call" | custom-call | flops 1000000000 | bytes 8388608 | tf_op jit(solution)/shard_map/write/pallas_call | solution.py:202
  28.3 3.0 %all-to-all-done.1 = bf16[32,16,128]{2,1,0:T(8,128)(2,1)S(1)} async-done(((bf16[32,16,128]{2,1,0:T(8,128)(2,1)}), bf16[32,16,128]{2,1,0:T(8,128)(2,1)S(1)}, u32[]{:S(2)}, u32[]{:S(2)}) %all-to-all-start.1) | async-done | bytes 131104 | tf_op jit(solution)/shard_map/all_to_all | solution.py:199
  31.3 0.7 %copy.10 = bf16[512,128]{1,0:T(8,128)(2,1)} copy(bf16[512,128]{1,0:T(8,128)(2,1)S(1)} %bitcast.3) | data formatting | bytes 262144
Async XLA Ops:
  0.6 17.3 %copy-start = (f32[4096,128]{1,0:T(8,128)S(1)}, f32[4096,128]{1,0:T(8,128)}, u32[]{:S(2)}) copy-start(f32[4096,128]{1,0:T(8,128)} %table_hbm.1) | copy-start | bytes 6291460
  0.6 17.2 %copy-start.1 = (f32[4096,128]{1,0:T(8,128)S(1)}, f32[4096,128]{1,0:T(8,128)}, u32[]{:S(2)}) copy-start(f32[4096,128]{1,0:T(8,128)} %accum_hbm.1) | copy-start | bytes 6291460
  20.4 10.8 %all-to-all-start.1 = ((bf16[32,16,128]{2,1,0:T(8,128)(2,1)}), bf16[32,16,128]{2,1,0:T(8,128)(2,1)S(1)}, u32[]{:S(2)}, u32[]{:S(2)}) async-start(bf16[32,16,128]{2,1,0:T(8,128)(2,1)} %bitcast.1), calls=%async_computation.1 | async-start | bytes 262144 | tf_op jit(solution)/shard_map/all_to_all | solution.py:199

commit v4 on v3

--- a/solution.py
+++ b/solution.py
@@ -11,6 +11,8 @@
 epsilon = 1e-08
 
 LANES = 128
+SUBLANES = 8
+GROUP = 16
 TAG_ROWS = 8
 DIGIT = 256
 SLOT_BLOCK = 512
@@ -59,68 +61,112 @@
     ]
 
 
+def gather_ids(cap, axes, got_ref, id_rows, id_smem, sem):
+    n_src = got_ref.shape[0]
+    per = LANES // cap
+    mine = lax.rem(lax.axis_index(axes), per)
+    lane = lax.broadcasted_iota(jnp.int32, (TAG_ROWS, LANES), 1)
+    own = lane // cap == mine
+    ids, weights = [], []
+    for r in range(n_src // per):
+        tile = jnp.zeros((TAG_ROWS, LANES), jnp.float32)
+        for k in range(per):
+            tag = got_ref[r * per + k, cap : cap + TAG_ROWS, :].astype(jnp.float32)
+            shift = lax.rem(k - mine + per, per) * cap
+            tile = tile + pltpu.roll(jnp.where(own, tag, 0.0), shift, 1)
+        row = tile[0:1] * DIGIT + tile[1:2]
+        id_rows[r : r + 1] = row.astype(jnp.int32)
+        ids.append(row)
+        weights.append(tile[2:3])
+    copy = pltpu.make_async_copy(id_rows, id_smem, sem)
+    copy.start()
+    return jnp.concatenate(ids, axis=1), jnp.concatenate(weights, axis=1), copy
+
+
+def each_slot(n, body):
+    block = min(SLOT_BLOCK, n)
+
+    def one_block(b):
+        for k in range(block):
+            s = b * block + k
+            body(s, s // LANES, s % LANES)
+
+    if n == block:
+        one_block(0)
+    else:
+
+        def step(s, carry):
+            body(s, s // LANES, lax.rem(s, LANES))
+            return carry
+
+        lax.fori_loop(0, n, step, 0, unroll=32)
+
+
 def slots_kernel(
     cap, axes, got_ref, table_ref, accum_ref, reply_ref, new_t_ref, new_a_ref, ids_ref,
-    id_smem, picked_t, picked_a, sem_i,
+    id_smem, sums, sem_i,
 ):
     n_src, _, width = got_ref.shape
     n = n_src * cap
+    row_f, weight_row, ids_copy = gather_ids(cap, axes, got_ref, ids_ref, id_smem, sem_i)
     per = LANES // cap
     first = lax.rem(lax.axis_index(axes), per) * cap
     lane = lax.broadcasted_iota(jnp.int32, (n_src, cap, LANES), 2)
     slot = lax.broadcasted_iota(jnp.int32, (n_src, cap, LANES), 1)
     mine = lane == slot + first
     tags = got_ref[:, cap : cap + TAG_ROWS, :].astype(jnp.float32)
-
-    def spread(i):
+    ones = jnp.ones((LANES, LANES), jnp.bfloat16)
+    f32 = jnp.float32
+
+    def down(i):
         own = jnp.where(mine, tags[:, i : i + 1, :], 0.0)
-        return own.reshape(n, LANES).astype(jnp.bfloat16)
-
-    upper, lower, weight = spread(0), spread(1), spread(2)
-    ones = jnp.ones((LANES, LANES), jnp.bfloat16)
-    one_row = jnp.ones((8, LANES), jnp.bfloat16)
-    f32 = jnp.float32
-
-    def down(x):
-        return jnp.dot(x, ones, preferred_element_type=f32)
-
-    def across(x):
-        return lax.dot_general(one_row, x, (((1,), (1,)), ((), ())), preferred_element_type=f32)
-
-    row_f = across(upper) * DIGIT + across(lower)
-    ids_ref[...] = row_f.astype(jnp.int32)
-    ids_copy = pltpu.make_async_copy(ids_ref.at[pl.ds(0, 1)], id_smem, sem_i)
-    ids_copy.start()
-    column = down(upper) * DIGIT + down(lower)
-    row_f, weight_row = row_f[0:1], across(weight)[0:1]
+        own = own.reshape(n, LANES).astype(jnp.bfloat16)
+        return jnp.dot(own, ones, preferred_element_type=f32)
+
+    column = down(0) * DIGIT + down(1)
     deltas = got_ref[:, 0:cap, :].reshape(n, width)
     values = jnp.concatenate([deltas, jnp.ones((n, LANES), jnp.bfloat16)], axis=1)
     block = min(SLOT_BLOCK, n)
-    sums = []
     for b in range(n // block):
         mark = jnp.concatenate([column[b * block : (b + 1) * block]] * (n // LANES), axis=1)
         weighted = jnp.where(mark == row_f, weight_row, 0.0).astype(jnp.bfloat16)
-        sums.append(jnp.dot(weighted, values, preferred_element_type=f32))
+        sums[b * block : (b + 1) * block] = jnp.dot(weighted, values, preferred_element_type=f32)
     ids_copy.wait()
-
-    def pick_t(s, carry):
-        picked_t[pl.ds(s, 1), :] = table_ref[pl.ds(id_smem[0, s], 1), :]
-        return carry
-
-    def pick_a(s, carry):
-        picked_a[pl.ds(s, 1), :] = accum_ref[pl.ds(id_smem[0, s], 1), :]
-        return carry
-
-    lax.fori_loop(0, n, pick_t, 0, unroll=32)
-    lax.fori_loop(0, n, pick_a, 0, unroll=32)
-    for b in range(n // block):
-        part = pl.ds(b * block, block)
-        grad = sums[b][:, 0:width] / jnp.maximum(sums[b][:, width : width + LANES], 1.0)
-        next_a = picked_a[part] + grad * grad
-        next_t = picked_t[part] - learn_rate * grad / (jnp.sqrt(next_a) + epsilon)
-        new_a_ref[part] = next_a
-        new_t_ref[part] = next_t
-        reply_ref[part] = next_t.astype(jnp.bfloat16)
+    sub = lax.broadcasted_iota(jnp.int32, (SUBLANES, width), 0)
+
+    def rows_at(ref, ids):
+        rows = jnp.broadcast_to(ref[pl.ds(ids[0], 1), :], (SUBLANES, width))
+        for k in range(1, SUBLANES):
+            row = jnp.broadcast_to(ref[pl.ds(ids[k], 1), :], (SUBLANES, width))
+            rows = jnp.where(sub == k, row, rows)
+        return rows
+
+    def update(g):
+        start = g * GROUP
+        lane = start % LANES if isinstance(g, int) else lax.rem(start, LANES)
+        fresh = []
+        for half in range(GROUP // SUBLANES):
+            at = half * SUBLANES
+            ids = [id_smem[start // LANES, lane + at + k] for k in range(SUBLANES)]
+            part = pl.ds(start + at, SUBLANES)
+            grad = sums[part, 0:width] / jnp.maximum(sums[part, width : width + LANES], 1.0)
+            next_a = rows_at(accum_ref, ids) + grad * grad
+            next_t = rows_at(table_ref, ids) - learn_rate * grad / (jnp.sqrt(next_a) + epsilon)
+            new_a_ref[part] = next_a
+            new_t_ref[part] = next_t
+            fresh.append(next_t)
+        reply_ref[pl.ds(start, GROUP)] = jnp.concatenate(fresh, axis=0).astype(jnp.bfloat16)
+
+    if n == block:
+        for g in range(n // GROUP):
+            update(g)
+    else:
+
+        def step(g, carry):
+            update(g)
+            return carry
+
+        lax.fori_loop(0, n // GROUP, step, 0, unroll=2)
 
 
 def write_kernel(
@@ -130,22 +176,18 @@
     loads = copies(table_hbm, tab, sem_t) + copies(accum_hbm, acc, sem_a)
     for load in loads:
         load.start()
-    ids_copy = pltpu.make_async_copy(ids_ref.at[pl.ds(0, 1)], id_smem, sem_i)
+    ids_copy = pltpu.make_async_copy(ids_ref, id_smem, sem_i)
     ids_copy.start()
     ids_copy.wait()
     for load in loads:
         load.wait()
 
-    def put_t(s, carry):
-        tab[pl.ds(id_smem[0, s], 1), :] = new_t_ref[pl.ds(s, 1), :]
-        return carry
-
-    def put_a(s, carry):
-        acc[pl.ds(id_smem[0, s], 1), :] = new_a_ref[pl.ds(s, 1), :]
-        return carry
-
-    lax.fori_loop(0, new_t_ref.shape[0], put_t, 0, unroll=32)
-    lax.fori_loop(0, new_t_ref.shape[0], put_a, 0, unroll=32)
+    def put(s, row, lane):
+        v = id_smem[row, lane]
+        tab[pl.ds(v, 1), :] = new_t_ref[pl.ds(s, 1), :]
+        acc[pl.ds(v, 1), :] = new_a_ref[pl.ds(s, 1), :]
+
+    each_slot(new_t_ref.shape[0], put)
     stores = copies(tab, out_t, sem_t) + copies(acc, out_a, sem_a)
     for store in stores:
         store.start()
@@ -185,13 +227,13 @@
         functools.partial(slots_kernel, cap, axes),
         out_shape=(
             jax.ShapeDtypeStruct((n, width), jnp.bfloat16), rows, rows,
-            jax.ShapeDtypeStruct((8, n), jnp.int32),
+            jax.ShapeDtypeStruct((n // LANES, LANES), jnp.int32),
         ),
         in_specs=[vmem] * 3,
         out_specs=(vmem,) * 4,
         scratch_shapes=[
-            pltpu.SMEM((1, n), jnp.int32), pltpu.VMEM((n, width), f32),
-            pltpu.VMEM((n, width), f32), pltpu.SemaphoreType.DMA,
+            pltpu.SMEM((n // LANES, LANES), jnp.int32),
+            pltpu.VMEM((n, width + LANES), f32), pltpu.SemaphoreType.DMA,
         ],
         compiler_params=pltpu.CompilerParams(vmem_limit_bytes=slots_vmem),
         name="slots",
@@ -206,7 +248,7 @@
         ),
         in_specs=[vmem, vmem, vmem, hbm, hbm],
         out_specs=(hbm, hbm),
-        scratch_shapes=[pltpu.SMEM((1, n), jnp.int32)] + held + [
+        scratch_shapes=[pltpu.SMEM((n // LANES, LANES), jnp.int32)] + held + [
             pltpu.SemaphoreType.DMA((COPIES,)), pltpu.SemaphoreType.DMA((COPIES,)),
             pltpu.SemaphoreType.DMA,
         ],

time: 32.2 us -> 31.5 us (0.978)
  Pallas kernels: 8.86 us -> 7.69 us
  waiting for transfers between devices: 3.02 us -> 3.56 us
    pallas_call x1, Pallas kernels: 2.55 us -> 1.92 us  [on_device(): pl.pallas_call(functools.partial(slots_kernel, cap, axes), out_shape=(jax...]
    all_to_all x1, waiting for transfers between devices: 3.02 us -> 3.56 us  [on_device(): lax.all_to_all(replies.reshape(n_dest, cap, width), axes, split_axis=0, c...]
    pallas_call x1, Pallas kernels: 5.18 us -> 4.63 us  [on_device(): pl.pallas_call(write_kernel, out_shape=(jax.ShapeDtypeStruct(table.shape,...]
  transfers between devices with their start and end apart: 1 -> 1, of which waited for: 1 -> 1; matrix products, arithmetic and copies ran while one was open for 0% -> 0% of each run, Pallas kernels for 16% -> 15%
where the time goes in v4:
time: 31.5 us; the launch traced here: 31.3 us
  blocking collectives  16.1 us (51%)
  Pallas kernels  7.69 us (24%)
  waiting for transfers between devices  3.56 us (11%)
  starting transfers between devices  2.63 us (8%)
  between operations  0.68 us (2%)
  local copies, waits for them, and re-layouts  0.67 us (2%)
    all_to_all x1, blocking collectives, on_device(): got = lax.all_to_all(payload, axes, split_axis=0, concat_axis=0, tiled=True)  16.1 us
    pallas_call x1, Pallas kernels, on_device(): pl.pallas_call(write_kernel, out_shape=(jax.ShapeDtypeStruct(table.shape,...  4.63 us
    all_to_all x1, waiting for transfers between devices, on_device(): lax.all_to_all(replies.reshape(n_dest, cap, width), axes, split_axis=0, c...  3.56 us
    all_to_all x1, starting transfers between devices, on_device(): lax.all_to_all(replies.reshape(n_dest, cap, width), axes, split_axis=0, c...  2.63 us
    pallas_call x1, Pallas kernels, on_device(): pl.pallas_call(functools.partial(slots_kernel, cap, axes), out_shape=(jax...  1.92 us
    pallas_call x1, Pallas kernels, on_device(): pl.pallas_call(functools.partial(pack_kernel, cap), out_shape=jax.ShapeDt...  1.14 us
    unnamed x5, local copies, waits for them, and re-layouts  0.67 us
  transfers between devices with their start and end apart: 1, of which 1 were waited for; matrix products, arithmetic and copies ran while one was open for 0% of the time, Pallas kernels for 15%

profile of v4, /device:TPU:0, one launch (start us, length us, event | category | flops | bytes accessed | tf_op | source)
XLA Modules:
  0.0 31.3 jit_solution(1883589268935891604)
XLA Ops:
  0.6 0.0 copy-start
  0.6 0.0 copy-start.1
  0.7 1.1 %pack.1 = bf16[32,24,128]{2,1,0:T(8,128)(2,1)S(1)} custom-call(bf16[32,16,128]{2,1,0:T(8,128)(2,1)} %bitcast.4, s32[512]{0:T(512)} %ids_hbm.1, s32[512]{0:T(512)} %counts_hbm.1, s32[512]{0:T(512)} %live_hbm.1), custom_call_target="tpu_custom_call" | custom-call | flops 10000000000 | bytes 16777216 | tf_op jit(solution)/shard_map/pack/pallas_call | solution.py:213
  1.8 16.1 %all_to_all.10.got_ref = bf16[32,24,128]{2,1,0:T(8,128)(2,1)S(1)} all-to-all(bf16[32,24,128]{2,1,0:T(8,128)(2,1)S(1)} %pack.1), channel_id=1, replica_groups=mesh['aa'=4,'ba'=8] {'aa','ba'}, dimensions={0} | all-to-all | bytes 393216 | tf_op jit(solution)/shard_map/all_to_all | solution.py:223
  17.9 0.0 copy-done
  17.9 0.0 copy-done.1
  17.9 1.9 %slots.1 = (bf16[512,128]{1,0:T(8,128)(2,1)}, f32[512,128]{1,0:T(8,128)S(1)}, f32[512,128]{1,0:T(8,128)S(1)}, s32[4,128]{1,0:T(4,128)S(1)}) custom-call(bf16[32,24,128]{2,1,0:T(8,128)(2,1)S(1)} %all_to_all.10.got_ref, f32[4096,128]{1,0:T(8,128)S(1)} %copy-done, f32[4096,128]{1,0:T(8,128)S(1)} %copy-done.1), custom_call_target="tpu_custom_call" | custom-call | tf_op jit(solution)/shard_map/slots/pallas_call | solution.py:226
  19.8 2.6 %all-to-all-start.1 = ((bf16[32,16,128]{2,1,0:T(8,128)(2,1)}), bf16[32,16,128]{2,1,0:T(8,128)(2,1)S(1)}, u32[]{:S(2)}, u32[]{:S(2)}) async-start(bf16[32,16,128]{2,1,0:T(8,128)(2,1)} %bitcast.1), calls=%async_computation.1 | async-start | bytes 262144 | tf_op jit(solution)/shard_map/all_to_all | solution.py:241
  22.5 4.6 %write.1 = (f32[4096,128]{1,0:T(8,128)}, f32[4096,128]{1,0:T(8,128)}) custom-call(s32[4,128]{1,0:T(4,128)S(1)} %get-tuple-element.9.ids_ref, f32[512,128]{1,0:T(8,128)S(1)} %get-tuple-element.10.new_t_ref, f32[512,128]{1,0:T(8,128)S(1)} %get-tuple-element.11.new_a_ref, f32[4096,128]{1,0:T(8,128)} %table_hbm.1, f32[4096,128]{1,0:T(8,128)} %accum_hbm.1), custom_call_target="tpu_custom_call" | custom-call | flops 1000000000 | bytes 8388608 | tf_op jit(solution)/shard_map/write/pallas_call | solution.py:244
  27.1 3.6 %all-to-all-done.1 = bf16[32,16,128]{2,1,0:T(8,128)(2,1)S(1)} async-done(((bf16[32,16,128]{2,1,0:T(8,128)(2,1)}), bf16[32,16,128]{2,1,0:T(8,128)(2,1)S(1)}, u32[]{:S(2)}, u32[]{:S(2)}) %all-to-all-start.1) | async-done | bytes 131104 | tf_op jit(solution)/shard_map/all_to_all | solution.py:241
  30.7 0.7 %copy.10 = bf16[512,128]{1,0:T(8,128)(2,1)} copy(bf16[512,128]{1,0:T(8,128)(2,1)S(1)} %bitcast.3) | data formatting | bytes 262144
Async XLA Ops:
  0.6 17.3 %copy-start = (f32[4096,128]{1,0:T(8,128)S(1)}, f32[4096,128]{1,0:T(8,128)}, u32[]{:S(2)}) copy-start(f32[4096,128]{1,0:T(8,128)} %table_hbm.1) | copy-start | bytes 6291460
  0.6 17.2 %copy-start.1 = (f32[4096,128]{1,0:T(8,128)S(1)}, f32[4096,128]{1,0:T(8,128)}, u32[]{:S(2)}) copy-start(f32[4096,128]{1,0:T(8,128)} %accum_hbm.1) | copy-start | bytes 6291460
  19.8 10.8 %all-to-all-start.1 = ((bf16[32,16,128]{2,1,0:T(8,128)(2,1)}), bf16[32,16,128]{2,1,0:T(8,128)(2,1)S(1)}, u32[]{:S(2)}, u32[]{:S(2)}) async-start(bf16[32,16,128]{2,1,0:T(8,128)(2,1)} %bitcast.1), calls=%async_computation.1 | async-start | bytes 262144 | tf_op jit(solution)/shard_map/all_to_all | solution.py:241

commit v5 on v4

--- a/solution.py
+++ b/solution.py
@@ -1,4 +1,5 @@
 import functools
+import math
 
 import jax
 import jax.numpy as jnp
@@ -13,7 +14,8 @@
 LANES = 128
 SUBLANES = 8
 GROUP = 16
-TAG_ROWS = 8
+TAG_ROWS = 4
+TILE = 4
 DIGIT = 256
 SLOT_BLOCK = 512
 COPIES = 4
@@ -21,22 +23,31 @@
 PACK_VMEM = 8 * MIB
 
 
+def as_rows(ref):
+    n_dest, tiles, _, width = ref.shape
+    return ref.reshape(n_dest * tiles * TILE, width)
+
+
 def pack_kernel(
-    cap, deltas_hbm, ids_hbm, counts_hbm, live_hbm, out_ref, ids_ref, counts_ref, live_ref, sem
+    cap, order, deltas_hbm, ids_hbm, counts_hbm, live_hbm, out_ref,
+    deltas_ref, ids_ref, counts_ref, live_ref, sem, sem_d,
 ):
     per = LANES // cap
     n_dest = out_ref.shape[0]
+    rows = cap + TAG_ROWS
     loads = [
         pltpu.make_async_copy(ids_hbm, ids_ref, sem.at[0]),
         pltpu.make_async_copy(counts_hbm, counts_ref, sem.at[1]),
         pltpu.make_async_copy(live_hbm, live_ref, sem.at[2]),
-        pltpu.make_async_copy(deltas_hbm, out_ref.at[:, pl.ds(0, cap), :], sem.at[3]),
     ]
+    loads_d = copies(deltas_hbm, deltas_ref, sem_d)
+    for load in loads + loads_d:
+        load.start()
     for load in loads:
-        load.start()
-    for load in loads[:3]:
         load.wait()
+    out = as_rows(out_ref)
     sub = lax.broadcasted_iota(jnp.int32, (TAG_ROWS, LANES), 0)
+    place = sorted(range(n_dest), key=order.__getitem__)
     for r in range(n_dest // per):
         lanes = pl.ds(r * LANES, LANES)
         ids = ids_ref[lanes][None, :]
@@ -45,10 +56,14 @@
         lower = jnp.bitwise_and(ids, DIGIT - 1)
         tag = jnp.where(sub == 0, upper, jnp.where(sub == 1, lower, jnp.where(sub == 2, weight, 0)))
         tag = tag.astype(jnp.float32).astype(jnp.bfloat16)
-        out_ref[pl.ds(r * per, per), cap : cap + TAG_ROWS, :] = jnp.broadcast_to(
-            tag[None], (per, TAG_ROWS, LANES)
-        )
-    loads[3].wait()
+        for owner in range(r * per, (r + 1) * per):
+            k = place[owner]
+            out[k * rows + cap : (k + 1) * rows] = tag
+    for load in loads_d:
+        load.wait()
+    for k in range(n_dest):
+        owner = order[k]
+        out[k * rows : k * rows + cap] = deltas_ref[owner * cap : (owner + 1) * cap]
 
 
 def copies(src, dst, sem):
@@ -63,6 +78,8 @@
 
 def gather_ids(cap, axes, got_ref, id_rows, id_smem, sem):
     n_src = got_ref.shape[0]
+    got = as_rows(got_ref)
+    rows = cap + TAG_ROWS
     per = LANES // cap
     mine = lax.rem(lax.axis_index(axes), per)
     lane = lax.broadcasted_iota(jnp.int32, (TAG_ROWS, LANES), 1)
@@ -71,7 +88,8 @@
     for r in range(n_src // per):
         tile = jnp.zeros((TAG_ROWS, LANES), jnp.float32)
         for k in range(per):
-            tag = got_ref[r * per + k, cap : cap + TAG_ROWS, :].astype(jnp.float32)
+            p = r * per + k
+            tag = got[p * rows + cap : (p + 1) * rows].astype(jnp.float32)
             shift = lax.rem(k - mine + per, per) * cap
             tile = tile + pltpu.roll(jnp.where(own, tag, 0.0), shift, 1)
         row = tile[0:1] * DIGIT + tile[1:2]
@@ -106,25 +124,27 @@
     cap, axes, got_ref, table_ref, accum_ref, reply_ref, new_t_ref, new_a_ref, ids_ref,
     id_smem, sums, sem_i,
 ):
-    n_src, _, width = got_ref.shape
+    n_src, _, _, width = got_ref.shape
     n = n_src * cap
+    got = as_rows(got_ref)
+    rows = cap + TAG_ROWS
     row_f, weight_row, ids_copy = gather_ids(cap, axes, got_ref, ids_ref, id_smem, sem_i)
     per = LANES // cap
     first = lax.rem(lax.axis_index(axes), per) * cap
-    lane = lax.broadcasted_iota(jnp.int32, (n_src, cap, LANES), 2)
-    slot = lax.broadcasted_iota(jnp.int32, (n_src, cap, LANES), 1)
+    lane = lax.broadcasted_iota(jnp.int32, (cap, LANES), 1)
+    slot = lax.broadcasted_iota(jnp.int32, (cap, LANES), 0)
     mine = lane == slot + first
-    tags = got_ref[:, cap : cap + TAG_ROWS, :].astype(jnp.float32)
+    tags = [got[p * rows + cap : (p + 1) * rows].astype(jnp.float32) for p in range(n_src)]
     ones = jnp.ones((LANES, LANES), jnp.bfloat16)
     f32 = jnp.float32
 
     def down(i):
-        own = jnp.where(mine, tags[:, i : i + 1, :], 0.0)
-        own = own.reshape(n, LANES).astype(jnp.bfloat16)
-        return jnp.dot(own, ones, preferred_element_type=f32)
+        own = [jnp.where(mine, tag[i : i + 1], 0.0).astype(jnp.bfloat16) for tag in tags]
+        return jnp.dot(jnp.concatenate(own, axis=0), ones, preferred_element_type=f32)
 
     column = down(0) * DIGIT + down(1)
-    deltas = got_ref[:, 0:cap, :].reshape(n, width)
+    deltas = [got[p * rows : p * rows + cap] for p in range(n_src)]
+    deltas = jnp.concatenate(deltas, axis=0)
     values = jnp.concatenate([deltas, jnp.ones((n, LANES), jnp.bfloat16)], axis=1)
     block = min(SLOT_BLOCK, n)
     for b in range(n // block):
@@ -195,6 +215,22 @@
         store.wait()
 
 
+def finish_kernel(cap, order, returned_ref, fresh_ref):
+    for k, owner in enumerate(order):
+        fresh_ref[owner * cap : (owner + 1) * cap] = returned_ref[k * cap : (k + 1) * cap]
+
+
+def block_order(n_dest):
+    step = -5 if math.gcd(n_dest, 5) == 1 else -1
+    return [step * k % n_dest for k in range(n_dest)]
+
+
+def exchange(blocks, axes, order):
+    return lax.all_to_all(
+        blocks, axes, split_axis=0, concat_axis=0, tiled=True, axis_index_groups=[order]
+    )
+
+
 def in_hbm(*arrays):
     return [pltpu.with_memory_space_constraint(x, pltpu.HBM) for x in arrays]
 
@@ -205,22 +241,27 @@
     width = deltas.shape[1]
     n = deltas.shape[0]
     cap = n // n_dest
+    order = block_order(n_dest)
     vmem = pl.BlockSpec(memory_space=pltpu.VMEM)
     hbm = pl.BlockSpec(memory_space=pltpu.HBM)
     f32 = jnp.float32
     slots_vmem = 16 * MIB if n <= SLOT_BLOCK else 60 * MIB
     write_vmem = 16 * MIB
     payload = pl.pallas_call(
-        functools.partial(pack_kernel, cap),
-        out_shape=jax.ShapeDtypeStruct((n_dest, cap + TAG_ROWS, width), jnp.bfloat16),
+        functools.partial(pack_kernel, cap, order),
+        out_shape=jax.ShapeDtypeStruct(
+            (n_dest, (cap + TAG_ROWS) // TILE, TILE, width), jnp.bfloat16
+        ),
         in_specs=[hbm] * 4,
         out_specs=vmem,
-        scratch_shapes=[pltpu.VMEM((n,), jnp.int32)] * 3 + [pltpu.SemaphoreType.DMA((4,))],
+        scratch_shapes=[pltpu.VMEM((n, width), jnp.bfloat16)]
+        + [pltpu.VMEM((n,), jnp.int32)] * 3
+        + [pltpu.SemaphoreType.DMA((3,)), pltpu.SemaphoreType.DMA((COPIES,))],
         compiler_params=pltpu.CompilerParams(vmem_limit_bytes=PACK_VMEM),
         cost_estimate=pl.CostEstimate(flops=10**10, transcendentals=0, bytes_accessed=2**24),
         name="pack",
-    )(*in_hbm(deltas.reshape(n_dest, cap, width), row_ids, sample_counts, live))
-    got = lax.all_to_all(payload, axes, split_axis=0, concat_axis=0, tiled=True)
+    )(*in_hbm(deltas, row_ids, sample_counts, live))
+    got = exchange(payload, axes, order)
     rows = jax.ShapeDtypeStruct((n, width), f32)
     held = [pltpu.VMEM(table.shape, f32), pltpu.VMEM(accum.shape, f32)]
     replies, new_t, new_a, ids = pl.pallas_call(
@@ -238,9 +279,7 @@
         compiler_params=pltpu.CompilerParams(vmem_limit_bytes=slots_vmem),
         name="slots",
     )(got, table, accum)
-    returned = lax.all_to_all(
-        replies.reshape(n_dest, cap, width), axes, split_axis=0, concat_axis=0, tiled=True
-    )
+    returned = exchange(replies.reshape(n_dest, cap, width), axes, order)
     new_table, new_accum = pl.pallas_call(
         write_kernel,
         out_shape=(
@@ -256,7 +295,15 @@
         compiler_params=pltpu.CompilerParams(vmem_limit_bytes=write_vmem),
         name="write",
     )(ids, new_t, new_a, *in_hbm(table, accum))
-    return (new_table, new_accum, returned.reshape(-1, width))
+    fresh = pl.pallas_call(
+        functools.partial(finish_kernel, cap, order),
+        out_shape=jax.ShapeDtypeStruct((n, width), jnp.bfloat16),
+        in_specs=[vmem],
+        out_specs=vmem,
+        compiler_params=pltpu.CompilerParams(vmem_limit_bytes=PACK_VMEM),
+        name="finish",
+    )(returned.reshape(-1, width))
+    return (new_table, new_accum, fresh)
 
 
 def solution(mesh):

time: 31.5 us -> 30.1 us (0.956)
  blocking collectives: 16.1 us -> 15.2 us
  waiting for transfers between devices: 3.56 us -> 2.89 us
  local copies, waits for them, and re-layouts: 0.67 us -> 0.01 us
  Pallas kernels: 7.69 us -> 8.34 us
    all_to_all x1, blocking collectives: 16.1 us -> 15.2 us  [exchange(): lax.all_to_all(blocks, axes, split_axis=0, concat_axis=0, tiled=True, axi...]
    all_to_all x1, waiting for transfers between devices: 3.56 us -> 2.89 us  [exchange(): lax.all_to_all(blocks, axes, split_axis=0, concat_axis=0, tiled=True, axi...]
    unnamed x5 -> x4, local copies, waits for them, and re-layouts: 0.67 us -> 0.01 us
    pallas_call x1 -> x2, Pallas kernels: 1.14 us -> 1.78 us  [the longest x1 1.12 us: on_device(): pl.pallas_call(functools.partial(pack_kernel, cap, order), out_shape=jax....]
where the time goes in v5:
time: 30.1 us; the launch traced here: 29.9 us
  blocking collectives  15.2 us (50%)
  Pallas kernels  8.34 us (28%)
  waiting for transfers between devices  2.89 us (10%)
  starting transfers between devices  2.85 us (9%)
  between operations  0.68 us (2%)
    all_to_all x1, blocking collectives, exchange(): lax.all_to_all(blocks, axes, split_axis=0, concat_axis=0, tiled=True, axi...  15.2 us
    pallas_call x1, Pallas kernels, on_device(): pl.pallas_call(write_kernel, out_shape=(jax.ShapeDtypeStruct(table.shape,...  4.63 us
    all_to_all x1, waiting for transfers between devices, exchange(): lax.all_to_all(blocks, axes, split_axis=0, concat_axis=0, tiled=True, axi...  2.89 us
    all_to_all x1, starting transfers between devices, exchange(): lax.all_to_all(blocks, axes, split_axis=0, concat_axis=0, tiled=True, axi...  2.85 us
    pallas_call x1, Pallas kernels, on_device(): pl.pallas_call(functools.partial(slots_kernel, cap, axes), out_shape=(jax...  1.93 us
    pallas_call x1, Pallas kernels, on_device(): pl.pallas_call(functools.partial(pack_kernel, cap, order), out_shape=jax....  1.12 us
    pallas_call x1, Pallas kernels, on_device(): pl.pallas_call(functools.partial(finish_kernel, cap, order), out_shape=ja...  0.66 us
  transfers between devices with their start and end apart: 1, of which 1 were waited for; matrix products, arithmetic and copies ran while one was open for 0% of the time, Pallas kernels for 15%

profile of v5, /device:TPU:0, one launch (start us, length us, event | category | flops | bytes accessed | tf_op | source)
XLA Modules:
  0.0 29.9 jit_solution(1722648170003571363)
XLA Ops:
  0.6 0.0 copy-start.1
  0.6 0.0 copy-start
  0.7 1.1 %pack.1 = bf16[32,5,4,128]{3,2,1,0:T(4,128)(2,1)S(1)} custom-call(bf16[512,128]{1,0:T(8,128)(2,1)} %deltas_hbm.1, s32[512]{0:T(512)} %ids_hbm.1, s32[512]{0:T(512)} %counts_hbm.1, s32[512]{0:T(512)} %live_hbm.1), custom_call_target="tpu_custom_call" | custom-call | flops 10000000000 | bytes 16777216 | tf_op jit(solution)/shard_map/pack/pallas_call | solution.py:250
  1.8 15.2 %all_to_all.10.got_ref = bf16[32,5,4,128]{3,2,1,0:T(4,128)(2,1)S(1)} all-to-all(bf16[32,5,4,128]{3,2,1,0:T(4,128)(2,1)S(1)} %pack.1), channel_id=1, replica_groups={{0,27,22,17,12,7,2,29,24,19,14,9,4,31,26,21,16,11,6,1,28,23,18,13,8,3,3..., dimensions={0} | all-to-all | bytes 327680 | tf_op jit(solution)/shard_map/all_to_all | solution.py:229
  16.9 0.0 copy-done.1
  16.9 0.0 copy-done
  16.9 1.9 %slots.1 = (bf16[512,128]{1,0:T(8,128)(2,1)}, f32[512,128]{1,0:T(8,128)S(1)}, f32[512,128]{1,0:T(8,128)S(1)}, s32[4,128]{1,0:T(4,128)S(1)}) custom-call(bf16[32,5,4,128]{3,2,1,0:T(4,128)(2,1)S(1)} %all_to_all.10.got_ref, f32[4096,128]{1,0:T(8,128)S(1)} %copy-done, f32[4096,128]{1,0:T(8,128)S(1)} %copy-done.1), custom_call_target="tpu_custom_call" | custom-call | tf_op jit(solution)/shard_map/slots/pallas_call | solution.py:267
  18.9 2.9 %all-to-all-start.1 = ((bf16[32,16,128]{2,1,0:T(8,128)(2,1)}), bf16[32,16,128]{2,1,0:T(8,128)(2,1)S(1)}, u32[]{:S(2)}, u32[]{:S(2)}) async-start(bf16[32,16,128]{2,1,0:T(8,128)(2,1)} %bitcast), calls=%async_computation.1 | async-start | bytes 262144 | tf_op jit(solution)/shard_map/all_to_all | solution.py:229
  21.7 4.6 %write.1 = (f32[4096,128]{1,0:T(8,128)}, f32[4096,128]{1,0:T(8,128)}) custom-call(s32[4,128]{1,0:T(4,128)S(1)} %get-tuple-element.9.ids_ref, f32[512,128]{1,0:T(8,128)S(1)} %get-tuple-element.10.new_t_ref, f32[512,128]{1,0:T(8,128)S(1)} %get-tuple-element.11.new_a_ref, f32[4096,128]{1,0:T(8,128)} %table_hbm.1, f32[4096,128]{1,0:T(8,128)} %accum_hbm.1), custom_call_target="tpu_custom_call" | custom-call | flops 1000000000 | bytes 8388608 | tf_op jit(solution)/shard_map/write/pallas_call | solution.py:283
  26.4 2.9 %all-to-all-done.1 = bf16[32,16,128]{2,1,0:T(8,128)(2,1)S(1)} async-done(((bf16[32,16,128]{2,1,0:T(8,128)(2,1)}), bf16[32,16,128]{2,1,0:T(8,128)(2,1)S(1)}, u32[]{:S(2)}, u32[]{:S(2)}) %all-to-all-start.1) | async-done | bytes 131104 | tf_op jit(solution)/shard_map/all_to_all | solution.py:229
  29.3 0.7 %finish.1 = bf16[512,128]{1,0:T(8,128)(2,1)} custom-call(bf16[512,128]{1,0:T(8,128)(2,1)S(1)} %bitcast.2), custom_call_target="tpu_custom_call" | custom-call | tf_op jit(solution)/shard_map/finish/pallas_call | solution.py:298
Async XLA Ops:
  0.6 16.3 %copy-start.1 = (f32[4096,128]{1,0:T(8,128)S(1)}, f32[4096,128]{1,0:T(8,128)}, u32[]{:S(2)}) copy-start(f32[4096,128]{1,0:T(8,128)} %accum_hbm.1) | copy-start | bytes 6291460
  0.6 16.3 %copy-start = (f32[4096,128]{1,0:T(8,128)S(1)}, f32[4096,128]{1,0:T(8,128)}, u32[]{:S(2)}) copy-start(f32[4096,128]{1,0:T(8,128)} %table_hbm.1) | copy-start | bytes 6291460
  18.9 10.4 %all-to-all-start.1 = ((bf16[32,16,128]{2,1,0:T(8,128)(2,1)}), bf16[32,16,128]{2,1,0:T(8,128)(2,1)S(1)}, u32[]{:S(2)}, u32[]{:S(2)}) async-start(bf16[32,16,128]{2,1,0:T(8,128)(2,1)} %bitcast), calls=%async_computation.1 | async-start | bytes 262144 | tf_op jit(solution)/shard_map/all_to_all | solution.py:229

commit v6 on v5

--- a/solution.py
+++ b/solution.py
@@ -220,9 +220,12 @@
         fresh_ref[owner * cap : (owner + 1) * cap] = returned_ref[k * cap : (k + 1) * cap]
 
 
-def block_order(n_dest):
-    step = -5 if math.gcd(n_dest, 5) == 1 else -1
-    return [step * k % n_dest for k in range(n_dest)]
+def block_order(n_first, n_second):
+    n_dest = n_first * n_second
+    order = [
+        (3 * k - k // n_second) % n_first * n_second + 3 * k % n_second for k in range(n_dest)
+    ]
+    return order if len(set(order)) == n_dest else list(range(n_dest))
 
 
 def exchange(blocks, axes, order):
@@ -241,7 +244,7 @@
     width = deltas.shape[1]
     n = deltas.shape[0]
     cap = n // n_dest
-    order = block_order(n_dest)
+    order = block_order(*(lax.axis_size(axis) for axis in axes))
     vmem = pl.BlockSpec(memory_space=pltpu.VMEM)
     hbm = pl.BlockSpec(memory_space=pltpu.HBM)
     f32 = jnp.float32

time: 30.1 us -> 29.9 us (level)
  transfers between devices with their start and end apart: 1 -> 1, of which waited for: 1 -> 1; matrix products, arithmetic and copies ran while one was open for 0% -> 0% of each run, Pallas kernels for 15% -> 16%
where the time goes in v6:
time: 29.9 us; the launch traced here: 29.7 us
  blocking collectives  14.9 us (50%)
  Pallas kernels  8.34 us (28%)
  starting transfers between devices  3.12 us (10%)
  waiting for transfers between devices  2.68 us (9%)
  between operations  0.68 us (2%)
    all_to_all x1, blocking collectives, exchange(): lax.all_to_all(blocks, axes, split_axis=0, concat_axis=0, tiled=True, axi...  14.9 us
    pallas_call x1, Pallas kernels, on_device(): pl.pallas_call(write_kernel, out_shape=(jax.ShapeDtypeStruct(table.shape,...  4.63 us
    all_to_all x1, starting transfers between devices, exchange(): lax.all_to_all(blocks, axes, split_axis=0, concat_axis=0, tiled=True, axi...  3.12 us
    all_to_all x1, waiting for transfers between devices, exchange(): lax.all_to_all(blocks, axes, split_axis=0, concat_axis=0, tiled=True, axi...  2.68 us
    pallas_call x1, Pallas kernels, on_device(): pl.pallas_call(functools.partial(slots_kernel, cap, axes), out_shape=(jax...  1.93 us
    pallas_call x1, Pallas kernels, on_device(): pl.pallas_call(functools.partial(pack_kernel, cap, order), out_shape=jax....  1.12 us
    pallas_call x1, Pallas kernels, on_device(): pl.pallas_call(functools.partial(finish_kernel, cap, order), out_shape=ja...  0.66 us
  transfers between devices with their start and end apart: 1, of which 1 were waited for; matrix products, arithmetic and copies ran while one was open for 0% of the time, Pallas kernels for 16%

profile of v6, /device:TPU:0, one launch (start us, length us, event | category | flops | bytes accessed | tf_op | source)
XLA Modules:
  0.0 29.7 jit_solution(4157315287213502674)
XLA Ops:
  0.6 0.0 copy-start.1
  0.6 0.0 copy-start
  0.7 1.1 %pack.1 = bf16[32,5,4,128]{3,2,1,0:T(4,128)(2,1)S(1)} custom-call(bf16[512,128]{1,0:T(8,128)(2,1)} %deltas_hbm.1, s32[512]{0:T(512)} %ids_hbm.1, s32[512]{0:T(512)} %counts_hbm.1, s32[512]{0:T(512)} %live_hbm.1), custom_call_target="tpu_custom_call" | custom-call | flops 10000000000 | bytes 16777216 | tf_op jit(solution)/shard_map/pack/pallas_call | solution.py:253
  1.8 14.9 %all_to_all.10.got_ref = bf16[32,5,4,128]{3,2,1,0:T(4,128)(2,1)S(1)} all-to-all(bf16[32,5,4,128]{3,2,1,0:T(4,128)(2,1)S(1)} %pack.1), channel_id=1, replica_groups={{0,27,22,9,4,31,18,13,24,19,14,1,28,23,10,5,16,11,6,25,20,15,2,29,8,3,3..., dimensions={0} | all-to-all | bytes 327680 | tf_op jit(solution)/shard_map/all_to_all | solution.py:232
  16.7 0.0 copy-done.1
  16.7 0.0 copy-done
  16.7 1.9 %slots.1 = (bf16[512,128]{1,0:T(8,128)(2,1)}, f32[512,128]{1,0:T(8,128)S(1)}, f32[512,128]{1,0:T(8,128)S(1)}, s32[4,128]{1,0:T(4,128)S(1)}) custom-call(bf16[32,5,4,128]{3,2,1,0:T(4,128)(2,1)S(1)} %all_to_all.10.got_ref, f32[4096,128]{1,0:T(8,128)S(1)} %copy-done, f32[4096,128]{1,0:T(8,128)S(1)} %copy-done.1), custom_call_target="tpu_custom_call" | custom-call | tf_op jit(solution)/shard_map/slots/pallas_call | solution.py:270
  18.6 3.1 %all-to-all-start.1 = ((bf16[32,16,128]{2,1,0:T(8,128)(2,1)}), bf16[32,16,128]{2,1,0:T(8,128)(2,1)S(1)}, u32[]{:S(2)}, u32[]{:S(2)}) async-start(bf16[32,16,128]{2,1,0:T(8,128)(2,1)} %bitcast), calls=%async_computation.1 | async-start | bytes 262144 | tf_op jit(solution)/shard_map/all_to_all | solution.py:232
  21.7 4.6 %write.1 = (f32[4096,128]{1,0:T(8,128)}, f32[4096,128]{1,0:T(8,128)}) custom-call(s32[4,128]{1,0:T(4,128)S(1)} %get-tuple-element.9.ids_ref, f32[512,128]{1,0:T(8,128)S(1)} %get-tuple-element.10.new_t_ref, f32[512,128]{1,0:T(8,128)S(1)} %get-tuple-element.11.new_a_ref, f32[4096,128]{1,0:T(8,128)} %table_hbm.1, f32[4096,128]{1,0:T(8,128)} %accum_hbm.1), custom_call_target="tpu_custom_call" | custom-call | flops 1000000000 | bytes 8388608 | tf_op jit(solution)/shard_map/write/pallas_call | solution.py:286
  26.4 2.7 %all-to-all-done.1 = bf16[32,16,128]{2,1,0:T(8,128)(2,1)S(1)} async-done(((bf16[32,16,128]{2,1,0:T(8,128)(2,1)}), bf16[32,16,128]{2,1,0:T(8,128)(2,1)S(1)}, u32[]{:S(2)}, u32[]{:S(2)}) %all-to-all-start.1) | async-done | bytes 131104 | tf_op jit(solution)/shard_map/all_to_all | solution.py:232
  29.0 0.7 %finish.1 = bf16[512,128]{1,0:T(8,128)(2,1)} custom-call(bf16[512,128]{1,0:T(8,128)(2,1)S(1)} %bitcast.2), custom_call_target="tpu_custom_call" | custom-call | tf_op jit(solution)/shard_map/finish/pallas_call | solution.py:301
Async XLA Ops:
  0.6 16.0 %copy-start.1 = (f32[4096,128]{1,0:T(8,128)S(1)}, f32[4096,128]{1,0:T(8,128)}, u32[]{:S(2)}) copy-start(f32[4096,128]{1,0:T(8,128)} %accum_hbm.1) | copy-start | bytes 6291460
  0.6 16.0 %copy-start = (f32[4096,128]{1,0:T(8,128)S(1)}, f32[4096,128]{1,0:T(8,128)}, u32[]{:S(2)}) copy-start(f32[4096,128]{1,0:T(8,128)} %table_hbm.1) | copy-start | bytes 6291460
  18.6 10.4 %all-to-all-start.1 = ((bf16[32,16,128]{2,1,0:T(8,128)(2,1)}), bf16[32,16,128]{2,1,0:T(8,128)(2,1)S(1)}, u32[]{:S(2)}, u32[]{:S(2)}) async-start(bf16[32,16,128]{2,1,0:T(8,128)(2,1)} %bitcast), calls=%async_computation.1 | async-start | bytes 262144 | tf_op jit(solution)/shard_map/all_to_all | solution.py:232

commit v7 on v6

--- a/solution.py
+++ b/solution.py
@@ -41,7 +41,7 @@
         pltpu.make_async_copy(live_hbm, live_ref, sem.at[2]),
     ]
     loads_d = copies(deltas_hbm, deltas_ref, sem_d)
-    for load in loads + loads_d:
+    for load in loads_d + loads:
         load.start()
     for load in loads:
         load.wait()
@@ -59,10 +59,11 @@
         for owner in range(r * per, (r + 1) * per):
             k = place[owner]
             out[k * rows + cap : (k + 1) * rows] = tag
-    for load in loads_d:
-        load.wait()
-    for k in range(n_dest):
-        owner = order[k]
+    part = n_dest // COPIES
+    for owner in range(n_dest):
+        if owner % part == 0:
+            loads_d[owner // part].wait()
+        k = place[owner]
         out[k * rows : k * rows + cap] = deltas_ref[owner * cap : (owner + 1) * cap]
 
 

time: 29.9 us -> 29.9 us (level)
  no operation moved by 1% of the time
where the time goes in v7:
time: 29.9 us; the launch traced here: 29.7 us
  blocking collectives  14.9 us (50%)
  Pallas kernels  8.29 us (28%)
  starting transfers between devices  3.12 us (10%)
  waiting for transfers between devices  2.68 us (9%)
  between operations  0.68 us (2%)
    all_to_all x1, blocking collectives, exchange(): lax.all_to_all(blocks, axes, split_axis=0, concat_axis=0, tiled=True, axi...  14.9 us
    pallas_call x1, Pallas kernels, on_device(): pl.pallas_call(write_kernel, out_shape=(jax.ShapeDtypeStruct(table.shape,...  4.63 us
    all_to_all x1, starting transfers between devices, exchange(): lax.all_to_all(blocks, axes, split_axis=0, concat_axis=0, tiled=True, axi...  3.12 us
    all_to_all x1, waiting for transfers between devices, exchange(): lax.all_to_all(blocks, axes, split_axis=0, concat_axis=0, tiled=True, axi...  2.68 us
    pallas_call x1, Pallas kernels, on_device(): pl.pallas_call(functools.partial(slots_kernel, cap, axes), out_shape=(jax...  1.93 us
    pallas_call x1, Pallas kernels, on_device(): pl.pallas_call(functools.partial(pack_kernel, cap, order), out_shape=jax....  1.06 us
    pallas_call x1, Pallas kernels, on_device(): pl.pallas_call(functools.partial(finish_kernel, cap, order), out_shape=ja...  0.66 us
  transfers between devices with their start and end apart: 1, of which 1 were waited for; matrix products, arithmetic and copies ran while one was open for 0% of the time, Pallas kernels for 16%

profile of v7, /device:TPU:0, one launch (start us, length us, event | category | flops | bytes accessed | tf_op | source)
XLA Modules:
  0.0 29.7 jit_solution(11944777175985510583)
XLA Ops:
  0.6 0.0 copy-start.1
  0.6 0.0 copy-start
  0.7 1.1 %pack.1 = bf16[32,5,4,128]{3,2,1,0:T(4,128)(2,1)S(1)} custom-call(bf16[512,128]{1,0:T(8,128)(2,1)} %deltas_hbm.1, s32[512]{0:T(512)} %ids_hbm.1, s32[512]{0:T(512)} %counts_hbm.1, s32[512]{0:T(512)} %live_hbm.1), custom_call_target="tpu_custom_call" | custom-call | flops 10000000000 | bytes 16777216 | tf_op jit(solution)/shard_map/pack/pallas_call | solution.py:254
  1.7 14.9 %all_to_all.10.got_ref = bf16[32,5,4,128]{3,2,1,0:T(4,128)(2,1)S(1)} all-to-all(bf16[32,5,4,128]{3,2,1,0:T(4,128)(2,1)S(1)} %pack.1), channel_id=1, replica_groups={{0,27,22,9,4,31,18,13,24,19,14,1,28,23,10,5,16,11,6,25,20,15,2,29,8,3,3..., dimensions={0} | all-to-all | bytes 327680 | tf_op jit(solution)/shard_map/all_to_all | solution.py:233
  16.6 0.0 copy-done.1
  16.6 0.0 copy-done
  16.6 1.9 %slots.1 = (bf16[512,128]{1,0:T(8,128)(2,1)}, f32[512,128]{1,0:T(8,128)S(1)}, f32[512,128]{1,0:T(8,128)S(1)}, s32[4,128]{1,0:T(4,128)S(1)}) custom-call(bf16[32,5,4,128]{3,2,1,0:T(4,128)(2,1)S(1)} %all_to_all.10.got_ref, f32[4096,128]{1,0:T(8,128)S(1)} %copy-done, f32[4096,128]{1,0:T(8,128)S(1)} %copy-done.1), custom_call_target="tpu_custom_call" | custom-call | tf_op jit(solution)/shard_map/slots/pallas_call | solution.py:271
  18.6 3.1 %all-to-all-start.1 = ((bf16[32,16,128]{2,1,0:T(8,128)(2,1)}), bf16[32,16,128]{2,1,0:T(8,128)(2,1)S(1)}, u32[]{:S(2)}, u32[]{:S(2)}) async-start(bf16[32,16,128]{2,1,0:T(8,128)(2,1)} %bitcast), calls=%async_computation.1 | async-start | bytes 262144 | tf_op jit(solution)/shard_map/all_to_all | solution.py:233
  21.7 4.6 %write.1 = (f32[4096,128]{1,0:T(8,128)}, f32[4096,128]{1,0:T(8,128)}) custom-call(s32[4,128]{1,0:T(4,128)S(1)} %get-tuple-element.9.ids_ref, f32[512,128]{1,0:T(8,128)S(1)} %get-tuple-element.10.new_t_ref, f32[512,128]{1,0:T(8,128)S(1)} %get-tuple-element.11.new_a_ref, f32[4096,128]{1,0:T(8,128)} %table_hbm.1, f32[4096,128]{1,0:T(8,128)} %accum_hbm.1), custom_call_target="tpu_custom_call" | custom-call | flops 1000000000 | bytes 8388608 | tf_op jit(solution)/shard_map/write/pallas_call | solution.py:287
  26.3 2.7 %all-to-all-done.1 = bf16[32,16,128]{2,1,0:T(8,128)(2,1)S(1)} async-done(((bf16[32,16,128]{2,1,0:T(8,128)(2,1)}), bf16[32,16,128]{2,1,0:T(8,128)(2,1)S(1)}, u32[]{:S(2)}, u32[]{:S(2)}) %all-to-all-start.1) | async-done | bytes 131104 | tf_op jit(solution)/shard_map/all_to_all | solution.py:233
  29.0 0.7 %finish.1 = bf16[512,128]{1,0:T(8,128)(2,1)} custom-call(bf16[512,128]{1,0:T(8,128)(2,1)S(1)} %bitcast.2), custom_call_target="tpu_custom_call" | custom-call | tf_op jit(solution)/shard_map/finish/pallas_call | solution.py:302
Async XLA Ops:
  0.6 16.0 %copy-start.1 = (f32[4096,128]{1,0:T(8,128)S(1)}, f32[4096,128]{1,0:T(8,128)}, u32[]{:S(2)}) copy-start(f32[4096,128]{1,0:T(8,128)} %accum_hbm.1) | copy-start | bytes 6291460
  0.6 16.0 %copy-start = (f32[4096,128]{1,0:T(8,128)S(1)}, f32[4096,128]{1,0:T(8,128)}, u32[]{:S(2)}) copy-start(f32[4096,128]{1,0:T(8,128)} %table_hbm.1) | copy-start | bytes 6291460
  18.6 10.4 %all-to-all-start.1 = ((bf16[32,16,128]{2,1,0:T(8,128)(2,1)}), bf16[32,16,128]{2,1,0:T(8,128)(2,1)S(1)}, u32[]{:S(2)}, u32[]{:S(2)}) async-start(bf16[32,16,128]{2,1,0:T(8,128)(2,1)} %bitcast), calls=%async_computation.1 | async-start | bytes 262144 | tf_op jit(solution)/shard_map/all_to_all | solution.py:233
